TPU v7x, 16 devices: a 4x2x1 block of a 4x4x8 slice. The times are simulated.
16 devices in a mesh: dp: 2 (over y, z), tp: 8 (over x, core).
Axes of the slice: x: 4, y: 2, z: 1, core: 2. Of those that a mesh axis runs over, the one named last changes fastest.
The devices are a block of a 4x4x8 slice.
Arguments:
- x_in: bfloat16 [4224, 3072], P(('dp', 'tp')), parts along dimension 0
- req_ids: int32 [4224], P('dp'), parts along dimension 0
- positions: int32 [4224], P('dp'), parts along dimension 0
- block_table: int32 [130, 256], P('dp'), parts along dimension 0
- ctx_len: int32 [130], P('dp'), parts along dimension 0
- k_pages: bfloat16 [8704, 16, 8, 128], P('dp', None, 'tp'), parts along dimension 0
- v_pages: bfloat16 [8704, 16, 8, 128], P('dp', None, 'tp'), parts along dimension 0
- w_q: bfloat16 [3072, 3072], P(None, 'tp')
- w_k: bfloat16 [3072, 1024], P(None, 'tp')
- w_v: bfloat16 [3072, 1024], P(None, 'tp')
- w_o: bfloat16 [3072, 3072], P('tp')
- w_gate: bfloat16 [3072, 8192], P(None, 'tp')
- w_up: bfloat16 [3072, 8192], P(None, 'tp')
- w_down: bfloat16 [8192, 3072], P('tp')
- g_attn: bfloat16 [3072], replicated
- g_mlp: bfloat16 [3072], replicated
Outputs:
- output 1: bfloat16 [4224, 3072], P(('dp', 'tp')), parts along dimension 0
- output 2: bfloat16 [8704, 16, 8, 128], P('dp', None, 'tp'), parts along dimension 0
- output 3: bfloat16 [8704, 16, 8, 128], P('dp', None, 'tp'), parts along dimension 0
There are 2 independent parts. A program takes and returns all parts, laid end to end along the dimension named above; an argument that names none is the same for every part.
All inputs are finite; a program needn't handle non-finite values.
Results may differ from a plain program's by a relative error of at most 0.0160456.
Values are sent between devices in bfloat16 or wider.
A program may use at most 768 MiB of HBM per device.

v0:
```python
import jax
import jax.numpy as jnp
from jax import lax
from jax.sharding import PartitionSpec as P, NamedSharding

EPS = 1e-5
THETA = 500000.0


def rms_norm(rows, gain):
    rows32 = rows.astype(jnp.float32)
    inv_rms = lax.rsqrt(jnp.mean(rows32 * rows32, axis=-1, keepdims=True) + EPS)
    return (rows32 * inv_rms * gain.astype(jnp.float32)).astype(jnp.bfloat16)


def rotary(vals, positions):
    half_dim = vals.shape[-1] // 2
    inv_freq = THETA ** (-jnp.arange(half_dim, dtype=jnp.float32) * 2.0 / vals.shape[-1])
    angles = positions.astype(jnp.float32)[:, None] * inv_freq[None, :]
    cosine = jnp.cos(angles)[:, None, :]
    sine_val = jnp.sin(angles)[:, None, :]
    vals32 = vals.astype(jnp.float32)
    first_half = vals32[..., :half_dim]
    second_half = vals32[..., half_dim:]
    return jnp.concatenate([first_half * cosine - second_half * sine_val, second_half * cosine + first_half * sine_val], axis=-1).astype(jnp.bfloat16)


def softmax_mix(scores, key_mask, form, values):
    scores = jnp.where(key_mask, scores, -1e30)
    row_max = jnp.max(scores, axis=-1, keepdims=True)
    weights = jnp.exp(scores - row_max)
    weight_sum = jnp.sum(weights, axis=-1, keepdims=True)
    mixed_out = jnp.einsum(form, weights.astype(jnp.bfloat16), values, preferred_element_type=jnp.float32)
    return (mixed_out / weight_sum).astype(jnp.bfloat16)


def qkv_cache(hidden, positions, req_ids, block_table, k_pages, v_pages, w_q, w_k, w_v):
    tokens = hidden.shape[0]
    head_dim = k_pages.shape[3]
    page_len = k_pages.shape[1]
    q_rows = jnp.dot(hidden, w_q, preferred_element_type=jnp.float32).astype(jnp.bfloat16).reshape(tokens, -1, head_dim)
    k_rows = jnp.dot(hidden, w_k, preferred_element_type=jnp.float32).astype(jnp.bfloat16).reshape(tokens, -1, head_dim)
    v_rows = jnp.dot(hidden, w_v, preferred_element_type=jnp.float32).astype(jnp.bfloat16).reshape(tokens, -1, head_dim)
    q_rows = rotary(q_rows, positions)
    k_rows = rotary(k_rows, positions)
    page_ids = block_table[req_ids, positions // page_len]
    slot_ids = positions % page_len
    k_cache = k_pages.at[page_ids, slot_ids].set(k_rows)
    v_cache = v_pages.at[page_ids, slot_ids].set(v_rows)
    return q_rows, k_cache, v_cache


def attend(q_rows, k_cache, v_cache, req_ids, positions, block_table, ctx_len):
    tokens, n_heads, head_dim = q_rows.shape
    kv_heads = k_cache.shape[2]
    group_rep = n_heads // kv_heads
    decode_len = block_table.shape[0] - 1
    chunk_len = tokens - decode_len
    key_span = block_table.shape[1] * k_cache.shape[1]
    attn_scale = head_dim ** -0.5
    last_key = jnp.minimum(positions, ctx_len[req_ids] - 1)
    key_pos = jnp.arange(key_span)
    chunk_row = lax.dynamic_index_in_dim(block_table, req_ids[0], axis=0, keepdims=False)
    chunk_keys = k_cache[chunk_row].reshape(key_span, kv_heads, head_dim)
    chunk_vals = v_cache[chunk_row].reshape(key_span, kv_heads, head_dim)
    chunk_q = q_rows[:chunk_len].reshape(chunk_len, kv_heads, group_rep, head_dim)
    chunk_scores = jnp.einsum('cgrd,tgd->gcrt', chunk_q, chunk_keys, preferred_element_type=jnp.float32) * attn_scale
    chunk_mask = (key_pos[None, :] <= last_key[:chunk_len, None])[None, :, None, :]
    chunk_out = softmax_mix(chunk_scores, chunk_mask, 'gcrt,tgd->gcrd', chunk_vals)
    chunk_out = jnp.transpose(chunk_out, (1, 0, 2, 3)).reshape(chunk_len, n_heads * head_dim)
    dec_rows = block_table[req_ids[chunk_len:]]
    dec_keys = k_cache[dec_rows].reshape(decode_len, key_span, kv_heads, head_dim)
    dec_vals = v_cache[dec_rows].reshape(decode_len, key_span, kv_heads, head_dim)
    dec_q = q_rows[chunk_len:].reshape(decode_len, kv_heads, group_rep, head_dim)
    dec_scores = jnp.einsum('ngrd,ntgd->ngrt', dec_q, dec_keys, preferred_element_type=jnp.float32) * attn_scale
    dec_mask = (key_pos[None, :] <= last_key[chunk_len:, None])[:, None, None, :]
    dec_out = softmax_mix(dec_scores, dec_mask, 'ngrt,ntgd->ngrd', dec_vals).reshape(decode_len, n_heads * head_dim)
    return jnp.concatenate([chunk_out, dec_out], axis=0)


def solution(mesh):
    row_spec = P(('dp', 'tp'), None)
    group_vec = P('dp')
    table_spec = P('dp', None)
    cache_spec = P('dp', None, 'tp', None)
    col_split = P(None, 'tp')
    row_split = P('tp', None)
    gain_spec = P(None)

    def device_layer(x_in, req_ids, positions, block_table, ctx_len, k_pages, v_pages, w_q, w_k, w_v, w_o, w_gate, w_up, w_down, g_attn, g_mlp):
        hidden = lax.all_gather(rms_norm(x_in, g_attn), 'tp', axis=0, tiled=True)
        q_rows, k_cache, v_cache = qkv_cache(hidden, positions, req_ids, block_table, k_pages, v_pages, w_q, w_k, w_v)
        attn_rows = attend(q_rows, k_cache, v_cache, req_ids, positions, block_table, ctx_len)
        attn_part = jnp.dot(attn_rows, w_o, preferred_element_type=jnp.float32).astype(jnp.bfloat16)
        attn_sum = lax.psum_scatter(attn_part, 'tp', scatter_dimension=0, tiled=True)
        mid_rows = (x_in.astype(jnp.float32) + attn_sum.astype(jnp.float32)).astype(jnp.bfloat16)
        hidden_mlp = lax.all_gather(rms_norm(mid_rows, g_mlp), 'tp', axis=0, tiled=True)
        gate_proj = jnp.dot(hidden_mlp, w_gate, preferred_element_type=jnp.float32)
        up_proj = jnp.dot(hidden_mlp, w_up, preferred_element_type=jnp.float32)
        act_rows = (jax.nn.silu(gate_proj) * up_proj).astype(jnp.bfloat16)
        down_part = jnp.dot(act_rows, w_down, preferred_element_type=jnp.float32).astype(jnp.bfloat16)
        down_sum = lax.psum_scatter(down_part, 'tp', scatter_dimension=0, tiled=True)
        x_out = (mid_rows.astype(jnp.float32) + down_sum.astype(jnp.float32)).astype(jnp.bfloat16)
        return x_out, k_cache, v_cache

    return jax.shard_map(device_layer, mesh=mesh, in_specs=(row_spec, group_vec, group_vec, table_spec, group_vec, cache_spec, cache_spec, col_split, col_split, col_split, row_split, col_split, col_split, row_split, gain_spec, gain_spec), out_specs=(row_spec, cache_spec, cache_spec), check_vma=False)
```

profile of v0, /device:TPU:112, one launch (start us, length us, event | category | flops | bytes accessed | tf_op | source)
XLA Modules:
  0.0 951.7 jit_solution(17906960728722035754)
XLA Ops:
  7.3 18.1 %copy.60 = bf16[4352,16,1,128]{3,1,2,0:T(8,128)(2,1)} copy(bf16[4352,16,1,128]{3,1,2,0:T(8,128)(2,1)} %param.21) | data formatting | bytes 35651584
  34.8 12.3 %gather_fusion = s32[2112]{0:T(1024)S(1)} fusion(s32[65]{0:T(128)S(1)} %copy-done.1, s32[3072]{0:T(1024)S(1)} %pad_clamp_fusion), kind=kCustom, calls=%fused_computation | custom fusion | bytes 25344 | tf_op jit(solution)/shard_map/gather | solution.py:61
  48.6 16.4 %gather_fusion.1 = s32[2112]{0:T(1024)S(1)} fusion(s32[65,256]{1,0:T(8,128)S(1)} %copy-done.2, s32[2112]{0:T(1024)S(1)} %get-tuple-element.17), kind=kCustom, calls=%fused_computation.1 | custom fusion | bytes 33792 | tf_op jit(solution)/shard_map/gather | solution.py:46
  72.9 10.2 %iota_compare_fusion = pred[2048,4096]{1,0:T(8,128)(4,1)} fusion(s32[2048]{0:T(1024)S(1)} %slice.54), kind=kLoop, calls=%fused_computation.16 | loop fusion | flops 8388608 | bytes 8396800 | tf_op jit(solution)/shard_map/le | solution.py:68
  83.0 19.0 %all-gather.3.cloned.1.call-done = bf16[2112,3072]{1,0:T(8,128)(2,1)} async-done(((bf16[264,3072]{1,0:T(8,128)(2,1)}), bf16[2112,3072]{1,0:T(8,128)(2,1)}) %all-gather.3.cloned.1.call-update) | async-done | bytes 12976144 | tf_op jit(solution)/shard_map/all_gather | solution.py:91
  102.0 8.8 fusion.9
  116.6 26.6 %scatter_fusion = bf16[69632,128]{1,0:T(8,128)(2,1)} fusion(bf16[69632,128]{1,0:T(8,128)(2,1)} %bitcast.57, s32[2112]{0:T(1024)S(1)} %broadcast_select_fusion, bf16[2112,128]{1,0:T(8,128)(2,1)} %copy.40), kind=kCustom, calls=%fused_computation.7 | custom fusion | bytes 1630464
  151.1 9.2 convolution_convert_fusion.3
  160.3 26.9 %scatter_fusion.1 = bf16[69632,128]{1,0:T(8,128)(2,1)} fusion(bf16[69632,128]{1,0:T(8,128)(2,1)} %bitcast.53, s32[2112]{0:T(1024)S(1)} %broadcast_select_fusion, bf16[2112,128]{1,0:T(8,128)(2,1)} %convolution_convert_fusion.3), kind=kCustom, calls=%fused_computation.8 | custom fusion | bytes 1630464
  195.1 132.1 %gather_fusion.5 = bf16[16384,16,128]{2,1,0:T(8,128)(2,1)} fusion(bf16[4352,16,128]{2,1,0:T(8,128)(2,1)} %bitcast.59, s32[16384]{0:T(1024)S(1)} %broadcast_clamp_fusion), kind=kCustom, calls=%fused_computation.5 | custom fusion | bytes 134283264 | tf_op jit(solution)/shard_map/gather | solution.py:72
  327.1 132.1 %gather_fusion.6 = bf16[16384,16,128]{2,1,0:T(8,128)(2,1)} fusion(bf16[4352,16,128]{2,1,0:T(8,128)(2,1)} %bitcast.55, s32[16384]{0:T(1024)S(1)} %broadcast_clamp_fusion), kind=kCustom, calls=%fused_computation.6 | custom fusion | bytes 134283264 | tf_op jit(solution)/shard_map/gather | solution.py:73
  459.3 11.8 %fusion.7 = f32[2112,384]{1,0:T(8,128)} fusion(bf16[2112,3072]{1,0:T(8,128)(2,1)} %all-gather.3.cloned.1.call-done, bf16[3072,384]{1,0:T(8,128)(2,1)} %param.23), kind=kOutput, calls=%fused_computation.29 | convolution fusion | flops 4984455168 | bytes 18579456 | tf_op jit(solution)/shard_map/dot_general | solution.py:41
  492.5 27.5 %fusion.57 = (f32[64,3]{1,0:T(8,128)S(1)}, f32[64,3,4096]{2,1,0:T(4,128)}) fusion(bf16[64,4096,128]{2,1,0:T(8,128)(2,1)} %bitcast.17, bf16[64,3,128]{2,0,1:T(8,128)(2,1)S(1)} %pad_maximum_fusion, pred[64,4096]{1,0:T(8,128)(4,1)S(1)} %copy-done.10), kind=kOutput, calls=%fused_computation.111 | convolution fusion | flops 203685696 | bytes 70566656 | tf_op jit(solution)/shard_map/ngrd,ntgd->ngrt/dot_general | solution.py:75
  523.8 22.9 %fusion.34 = bf16[64,3,128]{2,1,0:T(4,128)(2,1)S(1)} fusion(bf16[64,4096,128]{2,1,0:T(8,128)(2,1)} %bitcast.18, f32[64,3,4096]{2,1,0:T(4,128)S(1)} %copy-done.3, f32[64,3]{1,0:T(8,128)S(1)} %get-tuple-element.18, f32[64,3]{1,0:T(8,128)S(1)} %fusion.18), kind=kOutput, calls=%fused_computation.60 | convolution fusion | flops 202948608 | bytes 70305280 | tf_op jit(solution)/shard_map/ngrt,ntgd->ngrd/dot_general | solution.py:33
  547.5 38.8 %fusion = (f32[2048,3]{0,1:T(4,128)S(1)}, f32[2048,3,4096]{2,0,1:T(8,128)}) fusion(pred[2048,4096]{1,0:T(8,128)(4,1)} %iota_compare_fusion, bf16[4096,128,1]{1,0,2:T(8,128)(2,1)S(1)} %bitcast.63, bf16[2112,3,64]{2,0,1:T(8,128)(2,1)} %copy-done.8, bf16[2112,3,64]{2,0,1:T(8,128)(2,1)} %copy-done.9), kind=kOutput, calls=%fused_computation.11 | convolution fusion | flops 6521088000 | bytes 111747072 | tf_op jit(solution)/shard_map/cgrd,tgd->gcrt/dot_general | solution.py:67
  586.3 34.8 %fusion.1 = f32[2048,3]{0,1:T(4,128)S(1)} fusion(f32[2048,3,4096]{2,0,1:T(8,128)} %get-tuple-element.21, f32[2048,3]{0,1:T(4,128)S(1)} %get-tuple-element.20, pred[2048,4096]{1,0:T(8,128)(4,1)} %iota_compare_fusion), kind=kLoop, calls=%fused_computation.12 | loop fusion | flops 100657152 | bytes 109101056 | tf_op jit(solution)/shard_map/reduce_sum | solution.py:32
  621.2 37.7 %divide_convert_fusion = bf16[2048,3,128]{0,2,1:T(8,128)(2,1)S(1)} fusion(f32[2048,3]{0,1:T(4,128)S(1)} %fusion.1, bf16[4096,128,1]{1,0,2:T(8,128)(2,1)S(1)} %bitcast.62, f32[2048,3,4096]{2,0,1:T(8,128)} %get-tuple-element.21, f32[2048,3]{0,1:T(4,128)S(1)} %get-tuple-element.20, pred[2048,4096]{1,0:T(8,128)(4,1)} %iota_compare_fusion), kind=kOutput, calls=%fused_computation.47 | convolution fusion | flops 6544687104 | bytes 111722496 | tf_op jit(solution)/shard_map/gcrt,tgd->gcrd/dot_general | solution.py:33
  658.9 10.0 %convolution_convert_fusion.1 = bf16[2112,3072]{1,0:T(8,128)(2,1)} fusion(bf16[384,3072]{1,0:T(8,128)(2,1)S(1)} %copy-done, bf16[64,384]{0,1:T(8,128)(2,1)S(1)} %bitcast.65, bf16[2048,384]{0,1:T(8,128)(2,1)S(1)} %bitcast.67), kind=kOutput, calls=%fused_computation.18 | convolution fusion | flops 4992565248 | bytes 16957440 | tf_op jit(solution)/shard_map/dot_general | solution.py:94
  669.6 70.1 %reduce-scatter.3.cloned.1.call-done = bf16[264,3072]{1,0:T(8,128)(2,1)} async-done(((bf16[2112,3072]{1,0:T(8,128)(2,1)}), bf16[264,3072]{1,0:T(8,128)(2,1)}) %reduce-scatter.3.cloned.1.call-update) | async-done | bytes 1622032 | tf_op jit(solution)/shard_map/reduce_scatter | solution.py:95
  744.7 64.7 %all-gather.5.cloned.1.call-done = bf16[2112,3072]{1,0:T(8,128)(2,1)} async-done(((bf16[264,3072]{1,0:T(8,128)(2,1)}), bf16[2112,3072]{1,0:T(8,128)(2,1)}) %all-gather.5.cloned.1.call-update) | async-done | bytes 12976144 | tf_op jit(solution)/shard_map/all_gather | solution.py:97
  809.4 19.7 %fusion.58 = f32[2112,1024]{1,0:T(8,128)} fusion(bf16[2112,3072]{1,0:T(8,128)(2,1)} %all-gather.5.cloned.1.call-done, bf16[3072,1024]{1,0:T(8,128)(2,1)} %param.27), kind=kOutput, calls=%fused_computation.112 | convolution fusion | flops 13287555072 | bytes 27918336 | tf_op jit(solution)/shard_map/dot_general | solution.py:98
  829.1 20.6 %multiply_convert_fusion = bf16[2112,1024]{1,0:T(8,128)(2,1)} fusion(f32[2112,1024]{1,0:T(8,128)} %fusion.58, bf16[2112,3072]{1,0:T(8,128)(2,1)S(1)} %copy-done.20, bf16[3072,1024]{1,0:T(8,128)(2,1)} %param.28), kind=kOutput, calls=%fused_computation.19 | convolution fusion | flops 13300531200 | bytes 32243712 | tf_op jit(solution)/shard_map/dot_general | solution.py:99
  849.7 20.1 %convolution_convert_fusion = bf16[2112,3072]{1,0:T(8,128)(2,1)} fusion(bf16[2112,1024]{1,0:T(8,128)(2,1)} %multiply_convert_fusion, bf16[1024,3072]{1,0:T(8,128)(2,1)} %param.29), kind=kOutput, calls=%fused_computation.17 | convolution fusion | flops 13294043136 | bytes 23592960 | tf_op jit(solution)/shard_map/dot_general | solution.py:101
  869.8 70.7 %reduce-scatter.5.cloned.1.call-done = bf16[264,3072]{1,0:T(8,128)(2,1)} async-done(((bf16[2112,3072]{1,0:T(8,128)(2,1)}), bf16[264,3072]{1,0:T(8,128)(2,1)}) %reduce-scatter.5.cloned.1.call-update) | async-done | bytes 1622032 | tf_op jit(solution)/shard_map/reduce_scatter | solution.py:102
  (95 shorter events, 74.1 us)
Async XLA Ops:
  7.2 651.7 %copy-start = (bf16[384,3072]{1,0:T(8,128)(2,1)S(1)}, bf16[384,3072]{1,0:T(8,128)(2,1)}, u32[]{:S(2)}) copy-start(bf16[384,3072]{1,0:T(8,128)(2,1)} %param.26) | copy-start | bytes 7077892
  7.2 94.8 %all-gather.3.cloned.1.call-start = ((), (), s32[]{:S(2)}) async-start(), calls=%async_computation.2 | async-start | bytes 14598144 | tf_op jit(solution)/shard_map/all_gather | solution.py:91
  7.3 18.1 %copy-start.6 = (bf16[4352,16,1,128]{3,1,2,0:T(8,128)(2,1)S(1)}, bf16[4352,16,1,128]{3,1,2,0:T(8,128)(2,1)}, u32[]{:S(2)}) copy-start(bf16[4352,16,1,128]{3,1,2,0:T(8,128)(2,1)} %param.22) | copy-start | bytes 53477380
  25.4 6.5 copy-start.16
  25.4 6.5 copy-start.4
  31.9 2.3 copy-start.14
  31.9 2.9 copy-start.1
  34.1 705.6 %reduce-scatter.3.cloned.1.call-start = ((), (), s32[]{:S(2)}) async-start(), calls=%async_computation.3 | async-start | bytes 14598144 | tf_op jit(solution)/shard_map/reduce_scatter | solution.py:95
  34.8 12.3 %copy-start.15 = (s32[2112]{0:T(1024)S(1)}, s32[2112]{0:T(1024)}, u32[]{:S(2)}) copy-start(s32[2112]{0:T(1024)} %param.18) | copy-start | bytes 25348
  34.8 13.8 %copy-start.2 = (s32[65,256]{1,0:T(8,128)S(1)}, s32[65,256]{1,0:T(8,128)}, u32[]{:S(2)}) copy-start(s32[65,256]{1,0:T(8,128)} %param.19) | copy-start | bytes 199684
  48.6 18.0 %copy-start.18 = (s32[2]{0:T(128)S(1)}, s32[2]{0:T(128)}, u32[]{:S(2)}) copy-start(s32[2]{0:T(128)} %constant.78) | copy-start | bytes 28
  48.6 18.1 %copy-start.19 = (s32[2]{0:T(128)S(1)}, s32[2]{0:T(128)}, u32[]{:S(2)}) copy-start(s32[2]{0:T(128)} %constant.81) | copy-start | bytes 28
  490.7 1.2 copy-start.8
  490.7 1.7 copy-start.9
  490.8 1.7 copy-start.10
  519.9 3.8 copy-start.3
  523.8 23.7 %copy-start.12 = (bf16[256,16,128]{2,1,0:T(8,128)(2,1)S(1)}, bf16[256,16,128]{2,1,0:T(8,128)(2,1)}, u32[]{:S(2)}) copy-start(bf16[256,16,128]{2,1,0:T(8,128)(2,1)} %gather_fusion.2) | copy-start | bytes 3145732
  586.3 34.9 %copy-start.11 = (bf16[256,16,128]{2,1,0:T(8,128)(2,1)S(1)}, bf16[256,16,128]{2,1,0:T(8,128)(2,1)}, u32[]{:S(2)}) copy-start(bf16[256,16,128]{2,1,0:T(8,128)(2,1)} %gather_fusion.3) | copy-start | bytes 3145732
  621.2 37.7 %copy-start.13 = (bf16[64,3,128]{0,2,1:T(8,128)(2,1)S(1)}, bf16[64,3,128]{0,2,1:T(8,128)(2,1)}, u32[]{:S(2)}) copy-start(bf16[64,3,128]{0,2,1:T(8,128)(2,1)} %copy.48) | copy-start | bytes 147460
  669.0 140.4 %all-gather.5.cloned.1.call-start = ((), (), s32[]{:S(2)}) async-start(), calls=%async_computation.4 | async-start | bytes 14598144 | tf_op jit(solution)/shard_map/all_gather | solution.py:97
  739.7 2.7 copy-start.5
  739.7 2.9 copy-start.7
  744.6 195.9 %reduce-scatter.5.cloned.1.call-start = ((), (), s32[]{:S(2)}) async-start(), calls=%async_computation.5 | async-start | bytes 14598144 | tf_op jit(solution)/shard_map/reduce_scatter | solution.py:102
  809.4 19.7 %copy-start.20 = (bf16[2112,3072]{1,0:T(8,128)(2,1)S(1)}, bf16[2112,3072]{1,0:T(8,128)(2,1)}, u32[]{:S(2)}) copy-start(bf16[2112,3072]{1,0:T(8,128)(2,1)} %all-gather.5.cloned.1.call-done) | copy-start | bytes 38928388
  (1 other events, 0.7 us)
Sparse Core Ops, SparseCore 0:
  34.2 67.7 all-gather.2
  669.1 70.5 reduce-scatter.2
  744.8 64.5 all-gather.4
  869.9 70.5 reduce-scatter.4
where the time goes:
time: 956 us; the launch traced here: 952 us
  local copies, waits for them, and re-layouts  409 us (43%)
  matrix products  227 us (24%)
  waiting for transfers between devices  225 us (24%)
  other arithmetic  74.1 us (8%)
  between operations  16.5 us (2%)
    gather x1, local copies, waits for them, and re-layouts, attend(): v_cache[dec_rows].reshape(decode_len, key_span, kv_heads, head_dim)  132 us
    gather x1, local copies, waits for them, and re-layouts, attend(): k_cache[dec_rows].reshape(decode_len, key_span, kv_heads, head_dim)  132 us
    unnamed x49, local copies, waits for them, and re-layouts  87.2 us
    reduce_scatter x1, waiting for transfers between devices, device_layer(): lax.psum_scatter(down_part, 'tp', scatter_dimension=0, tiled=True)  70.7 us
    reduce_scatter x1, waiting for transfers between devices, device_layer(): lax.psum_scatter(attn_part, 'tp', scatter_dimension=0, tiled=True)  70.1 us
    all_gather x1, waiting for transfers between devices, device_layer(): lax.all_gather(rms_norm(mid_rows, g_mlp), 'tp', axis=0, tiled=True)  64.7 us
    dot_general x2, matrix products, softmax_mix(): jnp.einsum(form, weights.astype(jnp.bfloat16), values, preferred_element_...  60.6 us
    dot_general x1, matrix products, attend(): jnp.einsum('cgrd,tgd->gcrt', chunk_q, chunk_keys, preferred_element_type=...  38.8 us
  transfers between devices with their start and end apart: 4, of which 4 were waited for; matrix products, arithmetic and copies ran while one was open for 5% of the time, Pallas kernels for 0%

commit v1 on v0

v1 whole, which is shorter than its diff:
```python
import functools

import jax
import jax.numpy as jnp
from jax import lax
from jax.experimental import pallas as pl
from jax.experimental.pallas import tpu as pltpu
from jax.sharding import PartitionSpec as P

EPS = 1e-5
THETA = 500000.0
LOG2E = 1.4426950408889634
ANY = pl.BlockSpec(memory_space=pl.ANY)
SMEM = pl.BlockSpec(memory_space=pltpu.SMEM)
VMEM = pl.BlockSpec(memory_space=pltpu.VMEM)


def rms_norm(rows, gain):
    rows32 = rows.astype(jnp.float32)
    inv_rms = lax.rsqrt(jnp.mean(rows32 * rows32, axis=-1, keepdims=True) + EPS)
    return (rows32 * inv_rms * gain.astype(jnp.float32)).astype(jnp.bfloat16)


def cost(flops, nbytes):
    return pl.CostEstimate(flops=int(flops), bytes_accessed=int(nbytes), transcendentals=0)


def stage_kernel(dec_pages, pre_pages, parts, table, reqs, kp, vp, ko, vo, kd, vd, kc, vc,
                 kbuf, vbuf, stage, in_sem, out_sem, stage_sem):
    pool, page, _ = kbuf.shape
    step = pool // parts
    n_dec = kd.shape[0]
    chunk_len = reqs.shape[0] - n_dec
    span = dec_pages * page

    def copy_in(c, src, buf, i):
        return pltpu.make_async_copy(src.at[pl.ds(i * step, step)], buf.at[pl.ds(i * step, step)], in_sem.at[c, i])

    def copy_out(c, buf, dst, i):
        return pltpu.make_async_copy(buf.at[pl.ds(i * step, step)], dst.at[pl.ds(i * step, step)], out_sem.at[c, i])

    pairs = ((kp, kbuf, ko, kd, kc), (vp, vbuf, vo, vd, vc))
    for c, (src, buf, _, _, _) in enumerate(pairs):
        for i in range(parts):
            copy_in(c, src, buf, i).start()

    def put(slot, dst):
        return pltpu.make_async_copy(stage.at[slot], dst, stage_sem.at[slot])

    for c, (src, buf, dst, dec, pre) in enumerate(pairs):
        for i in range(parts):
            copy_in(c, src, buf, i).wait()
            copy_out(c, buf, dst, i).start()

        def gather(req, first, slot, buf=buf):
            for j in range(dec_pages):
                stage[slot, pl.ds(j * page, page), :] = buf[table[req, first + j]]

        for g in range(pre_pages // dec_pages):
            slot = g % 2
            if g >= 2 or c > 0:
                put(slot, pre.at[pl.ds(0, span)]).wait()
            gather(reqs[0], g * dec_pages, slot)
            put(slot, pre.at[pl.ds(g * span, span)]).start()

        def body(i, carry, dec=dec):
            slot = lax.rem(i, 2)
            put(slot, dec.at[0]).wait()
            gather(reqs[chunk_len + i], 0, slot)
            put(slot, dec.at[i]).start()
            return carry

        lax.fori_loop(0, n_dec, body, 0)
    for slot in range(2):
        put(slot, vd.at[0]).wait()
    for c, (_, buf, dst, _, _) in enumerate(pairs):
        for i in range(parts):
            copy_out(c, buf, dst, i).wait()


def stage_cache(table, reqs, kp, vp, n_dec, dec_pages, pre_pages):
    pool, page, head = kp.shape
    parts = 4
    bf = jnp.bfloat16
    dec = jax.ShapeDtypeStruct((n_dec, dec_pages * page, head), bf)
    pre = jax.ShapeDtypeStruct((pre_pages * page, head), bf)
    full = jax.ShapeDtypeStruct(kp.shape, bf)
    return pl.pallas_call(
        functools.partial(stage_kernel, dec_pages, pre_pages, parts),
        out_shape=[full, full, dec, dec, pre, pre],
        in_specs=[SMEM, SMEM, ANY, ANY],
        out_specs=[ANY] * 6,
        scratch_shapes=[
            pltpu.VMEM((pool, page, head), bf),
            pltpu.VMEM((pool, page, head), bf),
            pltpu.VMEM((2, dec_pages * page, head), bf),
            pltpu.SemaphoreType.DMA((2, parts)),
            pltpu.SemaphoreType.DMA((2, parts)),
            pltpu.SemaphoreType.DMA((2,)),
        ],
        compiler_params=pltpu.CompilerParams(vmem_limit_bytes=40 * 2**20),
        cost_estimate=cost(4e10, 1e8),
        name="stage_cache",
    )(table, reqs, kp, vp)


def qkv_kernel(head, n_q, h, w, cs, sn, q_out, k_out, v_out):
    cos, sin = cs[...], sn[...]
    x = jnp.dot(h[...], w[...], preferred_element_type=jnp.float32).astype(jnp.bfloat16)
    for n in range(n_q + 1):
        part = x[:, n * head:(n + 1) * head].astype(jnp.float32)
        val = (part * cos + pltpu.roll(part, head // 2, 1) * sin).astype(jnp.bfloat16)
        if n < n_q:
            q_out[n] = val
        else:
            k_out[...] = val
    v_out[...] = x[:, (n_q + 1) * head:]


def qkv(hidden, w, cos, sin, head):
    tokens, d = hidden.shape
    cols = w.shape[1]
    n_q = cols // head - 2
    blk = tokens // 4
    bf = jnp.bfloat16
    row = lambda c: pl.BlockSpec((blk, c), lambda i: (i, 0))
    return pl.pallas_call(
        functools.partial(qkv_kernel, head, n_q),
        grid=(tokens // blk,),
        out_shape=[
            jax.ShapeDtypeStruct((n_q, tokens, head), bf),
            jax.ShapeDtypeStruct((tokens, head), bf),
            jax.ShapeDtypeStruct((tokens, head), bf),
        ],
        in_specs=[row(d), pl.BlockSpec((d, cols), lambda i: (0, 0)), row(head), row(head)],
        out_specs=[pl.BlockSpec((n_q, blk, head), lambda i: (0, i, 0)), row(head), row(head)],
        compiler_params=pltpu.CompilerParams(vmem_limit_bytes=40 * 2**20),
        cost_estimate=cost(2 * tokens * d * cols, 2 * tokens * d),
        name="qkv",
    )(hidden, w, cos, sin)


def chunk_kernel(bq, bk, scale, q, kc, vc, kn, vn, out, acc, m_ref, l_ref):
    b = pl.program_id(0)
    n_q, _, head = q.shape
    rows = n_q * bq
    qq = q[...].reshape(rows, head)
    m_ref[...] = jnp.full_like(m_ref, -jnp.inf)
    l_ref[...] = jnp.zeros_like(l_ref)
    acc[...] = jnp.zeros_like(acc)

    def attend(keys, vals, masked):
        s = lax.dot_general(qq, keys, (((1,), (1,)), ((), ())), preferred_element_type=jnp.float32)
        if masked:
            i = lax.rem(lax.broadcasted_iota(jnp.int32, s.shape, 0), bq)
            j = lax.broadcasted_iota(jnp.int32, s.shape, 1)
            s = jnp.where(j <= i, s, -1e30)
        m_old = m_ref[...]
        m_new = jnp.maximum(m_old, jnp.max(s, axis=-1, keepdims=True))
        alpha = jnp.exp2((m_old - m_new) * scale)
        p = jnp.exp2((s - m_new[:, :1]) * scale)
        l_ref[...] = l_ref[...] * alpha + jnp.sum(p, axis=-1, keepdims=True)
        acc[...] = acc[...] * alpha + jnp.dot(p.astype(jnp.bfloat16), vals, preferred_element_type=jnp.float32)
        m_ref[...] = m_new

    def pre(t, carry):
        sl = pl.ds(pl.multiple_of(t * bk, bk), bk)
        attend(kc[sl, :], vc[sl, :], False)
        return carry

    lax.fori_loop(0, kc.shape[0] // bk, pre, 0)

    def new(t, carry):
        sl = pl.ds(pl.multiple_of(t * bq, bq), bq)
        attend(kn[sl, :], vn[sl, :], False)
        return carry

    lax.fori_loop(0, b, new, 0)
    sl = pl.ds(pl.multiple_of(b * bq, bq), bq)
    attend(kn[sl, :], vn[sl, :], True)
    o = (acc[...] / l_ref[...]).astype(jnp.bfloat16).reshape(n_q, bq, head)
    for n in range(n_q):
        out[:, n * head:(n + 1) * head] = o[n]


def chunk_attention(q, kc, vc, kn, vn, chunk_len):
    n_q, _, head = q.shape
    bq, bk = 256, 512
    scale = head ** -0.5 * LOG2E
    whole = lambda a: pl.BlockSpec((a.shape[0], head), lambda i: (0, 0))
    new = pl.BlockSpec((chunk_len, head), lambda i: (0, 0))
    pre_len = kc.shape[0]
    return pl.pallas_call(
        functools.partial(chunk_kernel, bq, bk, scale),
        grid=(chunk_len // bq,),
        out_shape=jax.ShapeDtypeStruct((chunk_len, n_q * head), jnp.bfloat16),
        in_specs=[pl.BlockSpec((n_q, bq, head), lambda i: (0, i, 0)), whole(kc), whole(vc), new, new],
        out_specs=pl.BlockSpec((bq, n_q * head), lambda i: (i, 0)),
        scratch_shapes=[pltpu.VMEM((n_q * bq, head), jnp.float32)] * 3,
        compiler_params=pltpu.CompilerParams(vmem_limit_bytes=32 * 2**20),
        cost_estimate=cost(4 * chunk_len * (pre_len + chunk_len // 2) * head * n_q, 4 * pre_len * head * 2),
        name="chunk_attention",
    )(q, kc, vc, kn, vn)


def decode_kernel(group, scale, n_q, chunk_len, pos, q, kd, vd, kn, vn, out):
    g = pl.program_id(0)
    _, pad, head = q.shape
    span = kd.shape[1]
    col = lax.broadcasted_iota(jnp.int32, (pad, span), 1)
    for r in range(group):
        p0 = pos[chunk_len + g * group + r]
        qr = q[r]
        self_k, self_v = kn[r].astype(jnp.float32), vn[r].astype(jnp.float32)
        s = lax.dot_general(qr, kd[r], (((1,), (1,)), ((), ())), preferred_element_type=jnp.float32)
        s_self = jnp.sum(qr.astype(jnp.float32) * self_k, axis=-1, keepdims=True)
        s = jnp.where(col < p0, s, -1e30)
        m = jnp.maximum(jnp.max(s, axis=-1, keepdims=True), s_self)
        p = jnp.exp2((s - m) * scale)
        p_self = jnp.exp2((s_self - m) * scale)
        l = jnp.sum(p, axis=-1, keepdims=True) + p_self
        o = jnp.dot(p.astype(jnp.bfloat16), vd[r], preferred_element_type=jnp.float32)
        o = o + p_self.astype(jnp.bfloat16).astype(jnp.float32) * self_v
        out[r] = (o / l).astype(jnp.bfloat16)


def decode_attention(pos, q, kd, vd, kn, vn, n_q):
    n_dec, pad, head = q.shape
    span = kd.shape[1]
    group = 8
    scale = head ** -0.5 * LOG2E
    blk = lambda n: pl.BlockSpec((group, n, head), lambda i: (i, 0, 0))
    return pl.pallas_call(
        functools.partial(decode_kernel, group, scale, n_q, pos.shape[0] - n_dec),
        grid=(n_dec // group,),
        out_shape=jax.ShapeDtypeStruct((n_dec, pad, head), jnp.bfloat16),
        in_specs=[SMEM, blk(pad), blk(span), blk(span), blk(1), blk(1)],
        out_specs=blk(pad),
        compiler_params=pltpu.CompilerParams(vmem_limit_bytes=32 * 2**20),
        cost_estimate=cost(2e10, 4 * n_dec * span * head),
        name="decode_attention",
    )(pos, q, kd, vd, kn, vn)


def update_kernel(pre_pages, table, reqs, pos, kn, vn, ki, vi, ko, vo, pages, sem, sem2):
    page = ki.shape[1]
    n_dec = pages.shape[1]
    chunk_len = reqs.shape[0] - n_dec
    chunk_pages = chunk_len // page
    req0 = reqs[0]
    pairs = ((kn, ki, ko), (vn, vi, vo))

    def dec_page(i):
        return table[reqs[chunk_len + i], pos[chunk_len + i] // page]

    for c, (new, old, out) in enumerate(pairs):

        def start(i, carry, c=c, old=old):
            pltpu.make_async_copy(old.at[dec_page(i)], pages.at[c, i], sem.at[c]).start()
            return carry

        lax.fori_loop(0, n_dec, start, 0)

        def put(i, carry, c=c, new=new, out=out):
            rows = pl.ds(pl.multiple_of(i * page, page), page)
            pltpu.make_async_copy(new.at[rows, :], out.at[table[req0, pre_pages + i]], sem2.at[c]).start()
            return carry

        lax.fori_loop(0, chunk_pages, put, 0, unroll=8)
    for c, (new, old, out) in enumerate(pairs):
        pltpu.make_async_copy(old.at[pl.ds(0, n_dec)], pages.at[c], sem.at[c]).wait()
        for i in range(n_dec):
            slot = lax.rem(pos[chunk_len + i], page)
            hit = lax.broadcasted_iota(jnp.int32, pages.shape[2:], 0) == slot
            row = jnp.broadcast_to(new[pl.ds(chunk_len + i, 1), :].astype(jnp.float32), pages.shape[2:])
            pages[c, i] = jnp.where(hit, row, pages[c, i].astype(jnp.float32)).astype(jnp.bfloat16)
    for c, (new, old, out) in enumerate(pairs):

        def back(i, carry, c=c, out=out):
            pltpu.make_async_copy(pages.at[c, i], out.at[dec_page(i)], sem.at[c]).start()
            return carry

        lax.fori_loop(0, n_dec, back, 0)
    for c, (new, old, out) in enumerate(pairs):
        pltpu.make_async_copy(pages.at[c], out.at[pl.ds(0, n_dec)], sem.at[c]).wait()
        pltpu.make_async_copy(new.at[pl.ds(0, chunk_len), :], new.at[pl.ds(0, chunk_len), :], sem2.at[c]).wait()


def update_cache(table, reqs, pos, kn, vn, k_all, v_all, n_dec, pre_pages):
    page, head = k_all.shape[1:]
    full = jax.ShapeDtypeStruct(k_all.shape, jnp.bfloat16)
    return pl.pallas_call(
        functools.partial(update_kernel, pre_pages),
        out_shape=[full, full],
        in_specs=[SMEM, SMEM, SMEM, VMEM, VMEM, ANY, ANY],
        out_specs=[ANY, ANY],
        input_output_aliases={5: 0, 6: 1},
        scratch_shapes=[
            pltpu.VMEM((2, n_dec, page, head), jnp.bfloat16),
            pltpu.SemaphoreType.DMA((2,)),
            pltpu.SemaphoreType.DMA((2,)),
        ],
        compiler_params=pltpu.CompilerParams(vmem_limit_bytes=16 * 2**20),
        cost_estimate=cost(4e9, 1e6),
        name="update_cache",
    )(table, reqs, pos, kn, vn, k_all, v_all)


def rope_tables(positions, head):
    half = head // 2
    inv_freq = THETA ** (-jnp.arange(half, dtype=jnp.float32) * 2.0 / head)
    angles = positions.astype(jnp.float32)[:, None] * inv_freq[None, :]
    cos, sin = jnp.cos(angles), jnp.sin(angles)
    return jnp.concatenate([cos, cos], axis=1), jnp.concatenate([-sin, sin], axis=1)


def ring_places(tp):
    chips = tp // 2
    me = lax.axis_index('tp')
    chip, core = me // 2, lax.rem(me, 2)
    sign = 1 - 2 * core
    peer = 2 * chip + 1 - core

    def chip_at(offset):
        return lax.rem(chip + sign * offset + 2 * chips, chips)

    return chip, core, peer, chip_at


def greet(*others):
    barrier = pltpu.get_barrier_semaphore()
    for other in others:
        pl.semaphore_signal(barrier, inc=1, device_id={'tp': other}, device_id_type=pl.DeviceIdType.MESH)
    pl.semaphore_wait(barrier, len(others))


def remote(src, dst, send, recv, to):
    return pltpu.make_async_remote_copy(src_ref=src, dst_ref=dst, send_sem=send, recv_sem=recv, device_id={'tp': to}, device_id_type=pl.DeviceIdType.MESH)


def proj_kernel(tp, parts, attn, w_o, x, g, mid_out, hid_out,
                psend, precv, ssend, rrecv, total, ps_sem, pr_sem, ss_sem, rr_sem):
    chips = tp // 2
    chip, core, peer, chip_at = ring_places(tp)
    nxt = 2 * chip_at(1) + core
    prv = 2 * chip_at(-1) + core
    wide = total.shape[2]
    greet(peer, nxt, prv)

    def to_peer(s, q):
        return remote(psend.at[s, q], precv.at[s, q], ps_sem.at[s, q], pr_sem.at[s, q], peer)

    def to_next(s, q):
        return remote(ssend.at[s, q], rrecv.at[s, q], ss_sem.at[s, q], rr_sem.at[s, q], nxt)

    def product(block, q):
        cols = pl.ds(pl.multiple_of(q * wide, wide), wide)
        return jnp.dot(attn[block], w_o[:, cols], preferred_element_type=jnp.float32)

    for s in range(chips):
        theirs = 2 * chip_at(s + 1) + 1 - core
        mine = 2 * chip_at(-(s + 1)) + core

        def give(q, carry, s=s, theirs=theirs):
            psend[s, q] = product(theirs, q).astype(jnp.bfloat16)
            to_peer(s, q).start()
            return carry

        lax.fori_loop(0, parts, give, 0)

        def take(q, carry, s=s, mine=mine):
            own = product(mine, q)
            to_peer(s, q).wait_recv()
            own = own + precv[s, q].astype(jnp.float32)
            if s > 0:
                to_next(s - 1, q).wait_recv()
                own = own + rrecv[s - 1, q].astype(jnp.float32)
            if s < chips - 1:
                ssend[s, q] = own.astype(jnp.bfloat16)
                to_next(s, q).start()
            else:
                total[q] = own
            return carry

        lax.fori_loop(0, parts, take, 0)

    for q in range(parts):
        cols = slice(q * wide, (q + 1) * wide)
        mid = (x[:, cols].astype(jnp.float32) + total[q].astype(jnp.bfloat16).astype(jnp.float32)).astype(jnp.bfloat16)
        mid_out[:, cols] = mid
        total[q] = mid.astype(jnp.float32)
    square = sum(jnp.sum(total[q] * total[q], axis=-1, keepdims=True) for q in range(parts))
    inv_rms = lax.rsqrt(square / (parts * wide) + EPS)
    for q in range(parts):
        cols = slice(q * wide, (q + 1) * wide)
        hid_out[:, cols] = (total[q] * inv_rms * g[:, cols].astype(jnp.float32)).astype(jnp.bfloat16)
    for s in range(chips):
        for q in range(parts):
            to_peer(s, q).wait_send()
            if s < chips - 1:
                to_next(s, q).wait_send()


def project(tp, attn, w_o, x, g):
    rows, d = x.shape
    parts = 3
    wide = d // parts
    chips = tp // 2
    bf = jnp.bfloat16
    dma = pltpu.SemaphoreType.DMA
    block = lambda n: pltpu.VMEM((n, parts, rows, wide), bf)
    out = jax.ShapeDtypeStruct((rows, d), bf)
    return pl.pallas_call(
        functools.partial(proj_kernel, tp, parts),
        out_shape=[out, out],
        in_specs=[VMEM] * 4,
        out_specs=[VMEM] * 2,
        scratch_shapes=[
            block(chips), block(chips), block(chips - 1), block(chips - 1),
            pltpu.VMEM((parts, rows, wide), jnp.float32),
            dma((chips, parts)), dma((chips, parts)), dma((chips - 1, parts)), dma((chips - 1, parts)),
        ],
        compiler_params=pltpu.CompilerParams(collective_id=1, has_side_effects=True, vmem_limit_bytes=60 * 2**20),
        cost_estimate=cost(6e10, 1e7),
        name="project",
    )(attn, w_o, x, g.reshape(1, d))


def mlp_kernel(tp, parts, hid, mid, w_gate, w_up, w_down, out,
               hbuf, gbuf, ubuf, dbuf, xbuf, act, acc, last, psend, precv, ssend, rrecv,
               in_sem, ag_s, ag_r, pg_s, pg_r, ps_sem, pr_sem, ss_sem, rr_sem):
    chips = tp // 2
    chip, core, peer, chip_at = ring_places(tp)
    nxt = 2 * chip_at(1) + core
    prv = 2 * chip_at(-1) + core
    _, rows, wide = acc.shape
    ff = gbuf.shape[1]
    tile = 256
    cut = 144
    halves = ((0, cut), (cut, rows - cut))
    loads = [pltpu.make_async_copy(a, b, in_sem.at[i]) for i, (a, b) in enumerate(
        ((hid, hbuf.at[0]), (w_gate, gbuf), (w_up, ubuf), (w_down, dbuf), (mid, xbuf)))]
    for load in loads:
        load.start()
    greet(peer, nxt, prv)

    def gather(j, i):
        first, n = halves[i]
        cut_rows = pl.ds(first, n)
        return remote(hbuf.at[j, cut_rows], hbuf.at[j + 1, cut_rows], ag_s.at[j, i], ag_r.at[j, i], nxt)

    def share(j):
        return remote(hbuf.at[j], hbuf.at[chips + j], pg_s.at[j], pg_r.at[j], peer)

    def to_peer(s, q):
        return remote(psend.at[s % 2, q], precv.at[s, q], ps_sem.at[s, q], pr_sem.at[s, q], peer)

    def to_next(s, q):
        return remote(ssend.at[s % 2, q], rrecv.at[s, q], ss_sem.at[s, q], rr_sem.at[s, q], nxt)

    def hidden_act(j):
        def body(t, carry):
            cols = pl.ds(pl.multiple_of(t * tile, tile), tile)
            gate = jnp.dot(hbuf[j], gbuf[:, cols], preferred_element_type=jnp.float32)
            up = jnp.dot(hbuf[j], ubuf[:, cols], preferred_element_type=jnp.float32)
            act[:, cols] = (gate * jax.nn.sigmoid(gate) * up).astype(jnp.bfloat16)
            return carry

        lax.fori_loop(0, ff // tile, body, 0)

    def down(q):
        cols = pl.ds(pl.multiple_of(q * wide, wide), wide)
        return jnp.dot(act[...], dbuf[:, cols], preferred_element_type=jnp.float32)

    def keep(j, dst):
        hidden_act(j)

        def body(q, carry):
            dst[q] = down(q)
            return carry

        lax.fori_loop(0, parts, body, 0)

    def give(j, s, before):
        hidden_act(j)

        def body(q, carry):
            if before is not None:
                to_peer(before, q).wait_send()
            psend[s % 2, q] = down(q).astype(jnp.bfloat16)
            to_peer(s, q).start()
            return carry

        lax.fori_loop(0, parts, body, 0)

    loads[0].wait()
    for i in range(2):
        gather(0, i).start()
    share(0).start()
    for load in loads[1:4]:
        load.wait()
    keep(0, last)
    share(0).wait_recv()
    end = chips - 1
    give(chips, end, None)
    for s in range(end):
        j = s + 1
        for i in range(2):
            gather(j - 1, i).wait_recv()
            if j < end:
                gather(j, i).start()
        share(j).start()
        keep(j, acc)
        share(j).wait_recv()
        give(chips + j, s, {0: None, 1: end, 2: 0}[s] if chips == 4 else None)

        def take(q, carry, s=s):
            to_peer(s, q).wait_recv()
            part = acc[q] + precv[s, q].astype(jnp.float32)
            if s > 0:
                to_next(s - 1, q).wait_recv()
                part = part + rrecv[s - 1, q].astype(jnp.float32)
            if s > 1:
                to_next(s - 2, q).wait_send()
            ssend[s % 2, q] = part.astype(jnp.bfloat16)
            to_next(s, q).start()
            return carry

        lax.fori_loop(0, parts, take, 0)

    loads[4].wait()
    for q in range(parts):
        cols = slice(q * wide, (q + 1) * wide)
        to_peer(end, q).wait_recv()
        part = last[q] + precv[end, q].astype(jnp.float32)
        to_next(end - 1, q).wait_recv()
        part = part + rrecv[end - 1, q].astype(jnp.float32)
        xbuf[:, cols] = (xbuf[:, cols].astype(jnp.float32) + part.astype(jnp.bfloat16).astype(jnp.float32)).astype(jnp.bfloat16)
    store = pltpu.make_async_copy(xbuf, out, in_sem.at[0])
    store.start()
    for j in range(chips):
        share(j).wait_send()
        if j < end:
            for i in range(2):
                gather(j, i).wait_send()
    for q in range(parts):
        to_peer(1, q).wait_send()
        to_peer(2, q).wait_send()
        for s in (end - 2, end - 1):
            to_next(s, q).wait_send()
    store.wait()


def mlp(tp, hid, mid, w_gate, w_up, w_down):
    rows, d = hid.shape
    ff = w_gate.shape[1]
    parts = 3
    wide = d // parts
    chips = tp // 2
    bf = jnp.bfloat16
    dma = pltpu.SemaphoreType.DMA
    block = lambda n: pltpu.VMEM((n, parts, rows, wide), bf)
    return pl.pallas_call(
        functools.partial(mlp_kernel, tp, parts),
        out_shape=jax.ShapeDtypeStruct((rows, d), bf),
        in_specs=[ANY] * 5,
        out_specs=ANY,
        scratch_shapes=[
            pltpu.VMEM((2 * chips, rows, d), bf),
            pltpu.VMEM((d, ff), bf), pltpu.VMEM((d, ff), bf), pltpu.VMEM((ff, d), bf),
            pltpu.VMEM((rows, d), bf), pltpu.VMEM((rows, ff), bf),
            pltpu.VMEM((parts, rows, wide), jnp.float32), pltpu.VMEM((parts, rows, wide), jnp.float32),
            block(2), block(chips), block(2), block(chips - 1),
            dma((5,)), dma((chips - 1, 2)), dma((chips - 1, 2)), dma((chips,)), dma((chips,)),
            dma((chips, parts)), dma((chips, parts)), dma((chips - 1, parts)), dma((chips - 1, parts)),
        ],
        compiler_params=pltpu.CompilerParams(collective_id=2, has_side_effects=True, vmem_limit_bytes=67043328),
        cost_estimate=cost(1e11, 2e7),
        name="mlp",
    )(hid, mid, w_gate, w_up, w_down)


def solution(mesh):
    tp = mesh.shape['tp']
    row_spec = P(('dp', 'tp'), None)
    group_vec = P('dp')
    table_spec = P('dp', None)
    cache_spec = P('dp', None, 'tp', None)
    col_split = P(None, 'tp')
    row_split = P('tp', None)
    gain_spec = P(None)

    def device_layer(x_in, req_ids, positions, block_table, ctx_len, k_pages, v_pages, w_q, w_k, w_v, w_o, w_gate, w_up, w_down, g_attn, g_mlp):
        pool, page, kv_heads, head = k_pages.shape
        tokens = positions.shape[0]
        n_dec = block_table.shape[0] - 1
        chunk_len = tokens - n_dec
        width = block_table.shape[1]
        pre_pages = width - chunk_len // page
        dec_pages = (pool - width) // n_dec
        n_q = w_q.shape[1] // head

        hidden = lax.all_gather(rms_norm(x_in, g_attn), 'tp', axis=0, tiled=True)
        ko, vo, kd, vd, kc, vc = stage_cache(block_table, req_ids, k_pages.reshape(pool, page, head), v_pages.reshape(pool, page, head), n_dec, dec_pages, pre_pages)
        cos, sin = rope_tables(positions, head)
        w_qkv = jnp.concatenate([w_q, w_k, w_v], axis=1)
        q, kn, vn = qkv(hidden, w_qkv, cos, sin, head)
        chunk_out = chunk_attention(q, kc, vc, kn, vn, chunk_len)
        q_dec = jnp.pad(jnp.transpose(q[:, chunk_len:], (1, 0, 2)), ((0, 0), (0, 8 - n_q), (0, 0)))
        dec_out = decode_attention(positions, q_dec, kd, vd, kn[chunk_len:, None], vn[chunk_len:, None], n_q)
        dec_out = dec_out[:, :n_q].reshape(n_dec, n_q * head)
        ko, vo = update_cache(block_table, req_ids, positions, kn, vn, ko, vo, n_dec, pre_pages)
        attn_rows = jnp.concatenate([chunk_out, dec_out], axis=0)
        mid_rows, hidden_mlp = project(tp, attn_rows.reshape(tp, tokens // tp, n_q * head), w_o, x_in, g_mlp)
        x_out = mlp(tp, hidden_mlp, mid_rows, w_gate, w_up, w_down)
        return x_out, ko.reshape(k_pages.shape), vo.reshape(v_pages.shape)

    return jax.shard_map(device_layer, mesh=mesh, in_specs=(row_spec, group_vec, group_vec, table_spec, group_vec, cache_spec, cache_spec, col_split, col_split, col_split, row_split, col_split, col_split, row_split, gain_spec, gain_spec), out_specs=(row_spec, cache_spec, cache_spec), check_vma=False)
```

time: 956 us -> 429 us (0.45)
  local copies, waits for them, and re-layouts: 409 us -> 26 us
  Pallas kernels: 0 us -> 375 us
  matrix products: 227 us -> 0 us
  waiting for transfers between devices: 225 us -> 0.07 us
  other arithmetic: 74.1 us -> 12.2 us
    pallas_call x0 -> x7, Pallas kernels: none -> 375 us  [the longest x1 112 us: mlp(): pl.pallas_call(functools.partial(mlp_kernel, tp, parts), out_shape=jax.Sh...]
    gather x7 -> x0, local copies, waits for them, and re-layouts: 309 us -> none  [the longest x1 132 us: attend(): v_cache[dec_rows].reshape(decode_len, key_span, kv_heads, head_dim)]
    dot_general x11 -> x0, matrix products: 227 us -> none  [the longest x2 60.6 us: softmax_mix(): jnp.einsum(form, weights.astype(jnp.bfloat16), values, preferred_element_...]
    reduce_scatter x2 -> x0, waiting for transfers between devices: 141 us -> none  [the longest x1 70.7 us: device_layer(): lax.psum_scatter(down_part, 'tp', scatter_dimension=0, tiled=True)]
    unnamed x49 -> x38, local copies, waits for them, and re-layouts: 87.2 us -> 14.9 us
    all_gather x1 -> x0, waiting for transfers between devices: 64.7 us -> none  [device_layer(): lax.all_gather(rms_norm(mid_rows, g_mlp), 'tp', axis=0, tiled=True)]
    reduce_sum x2 -> x0, other arithmetic: 38.7 us -> none  [softmax_mix(): weight_sum = jnp.sum(weights, axis=-1, keepdims=True)]
    all_gather x1, waiting for transfers between devices: 19 us -> 0.02 us  [device_layer(): hidden = lax.all_gather(rms_norm(x_in, g_attn), 'tp', axis=0, tiled=True)]
  transfers between devices with their start and end apart: 4 -> 1, of which waited for: 4 -> 0; matrix products, arithmetic and copies ran while one was open for 5% -> 2% of each run, Pallas kernels for 0% -> 16%
where the time goes in v1:
time: 429 us; the launch traced here: 428 us
  Pallas kernels  375 us (87%)
  local copies, waits for them, and re-layouts  26 us (6%)
  between operations  14.3 us (3%)
  other arithmetic  12.2 us (3%)
    pallas_call x1, Pallas kernels, mlp(): pl.pallas_call(functools.partial(mlp_kernel, tp, parts), out_shape=jax.Sh...  112 us
    pallas_call x1, Pallas kernels, chunk_attention(): pl.pallas_call(functools.partial(chunk_kernel, bq, bk, scale), grid=(chun...  85.7 us
    pallas_call x1, Pallas kernels, stage_cache(): pl.pallas_call(functools.partial(stage_kernel, dec_pages, pre_pages, part...  68.7 us
    pallas_call x1, Pallas kernels, project(): pl.pallas_call(functools.partial(proj_kernel, tp, parts), out_shape=[out,...  66.5 us
    pallas_call x1, Pallas kernels, decode_attention(): pl.pallas_call(functools.partial(decode_kernel, group, scale, n_q, pos.sh...  21.3 us
    unnamed x38, local copies, waits for them, and re-layouts  14.9 us
    pallas_call x1, Pallas kernels, qkv(): pl.pallas_call(functools.partial(qkv_kernel, head, n_q), grid=(tokens //...  13.1 us
    pallas_call x1, local copies, waits for them, and re-layouts, qkv(): pl.pallas_call(functools.partial(qkv_kernel, head, n_q), grid=(tokens //...  10.4 us
  transfers between devices with their start and end apart: 1, of which 0 were waited for; matrix products, arithmetic and copies ran while one was open for 2% of the time, Pallas kernels for 16%

profile of v1, /device:TPU:112, one launch (start us, length us, event | category | flops | bytes accessed | tf_op | source)
XLA Modules:
  0.0 428.1 jit_solution(9640437710601021657)
XLA Ops:
  7.3 0.8 convert_element_type.15
  8.1 1.8 fusion
  9.9 1.7 fusion.2
  12.3 3.8 fusion.3
  16.2 0.6 pad_maximum_fusion.2
  16.8 1.0 copy-done.13
  18.2 2.1 pad_maximum_fusion.w
  20.3 68.7 %stage_cache.1 = (bf16[4352,16,128]{2,1,0:T(8,128)(2,1)}, bf16[4352,16,128]{2,1,0:T(8,128)(2,1)}, bf16[64,1024,128]{2,1,0:T(8,128)(2,1)}, bf16[64,1024,128]{2,1,...) custom-call(s32[65,256]{1,0:T(8,128)S(1)} %copy-done.5, s32[2112]{0:T(1024)S(1)} %copy-done.9, ...), custom_call_target="tpu_custom_call" | custom-call | flops 40000000000 | bytes 100000000 | tf_op jit(solution)/shard_map/stage_cache/pallas_call | solution.py:88
  89.1 2.1 copy-done
  91.2 13.1 %qkv.1 = (bf16[3,2112,128]{2,1,0:T(8,128)(2,1)S(1)}, bf16[2112,128]{1,0:T(8,128)(2,1)S(1)}, bf16[2112,128]{1,0:T(8,128)(2,1)S(1)}) custom-call(bf16[2112,3072]{1,0:T(8,128)(2,1)} %all-gather.2.cloned.1.call-done.h, bf16[3072,640]{1,0:T(8,128)(2,1)S(1)} %copy-done, f32[2112,128]{1,0:T(8,128)S(1)} %get-tuple-element.38.cs, f32[2112,128]{1,0:T(8,128)S(1)} %get-tuple-element.39.sn), custom_call_target="tpu_custom_call" | custom-call | flops 8304721920 | bytes 12976128 | tf_op jit(solution)/shard_map/qkv/pallas_call | solution.py:127
  104.3 10.4 %copy.23 = bf16[3,2112,128]{2,0,1:T(4,128)(2,1)S(1)} copy(bf16[3,2112,128]{2,1,0:T(8,128)(2,1)S(1)} %get-tuple-element.16.q) | data formatting | bytes 3244032 | tf_op jit(solution)/shard_map/qkv/pallas_call | solution.py:127
  114.8 5.8 %copy-done.11 = bf16[64,1024,128]{2,1,0:T(8,128)(2,1)S(1)} copy-done((bf16[64,1024,128]{2,1,0:T(8,128)(2,1)S(1)}, bf16[64,1024,128]{2,1,0:T(8,128)(2,1)}, u32[]{:S(2)}) %copy-start.11) | copy-done | bytes 16777240
  120.6 21.3 %decode_attention.1 = bf16[64,8,128]{2,1,0:T(8,128)(2,1)S(1)} custom-call(s32[2112]{0:T(1024)S(1)} %copy-done.7, bf16[64,8,128]{2,1,0:T(8,128)(2,1)S(1)} %pad.4.q, bf16[64,1024,128]{2,1,0:T(8,128)(2,1)S(1)} %copy-done.11, bf16[64,1024,128]{2,1,0:T(8,128)(2,1)} %get-tuple-element.22.vd, bf16[64,1,128]{2,1,0:T(2,128)(2,1)S(1)} %copy.24.kn, ...), custom_call_target="tpu_custom_call" | custom-call | flops 20000000000 | bytes 33554432 | tf_op jit(solution)/shard_map/decode_attention/pallas_call | solution.py:233
  141.9 85.7 %chunk_attention.1 = bf16[2048,384]{1,0:T(8,128)(2,1)S(1)} custom-call(bf16[3,2112,128]{2,1,0:T(8,128)(2,1)S(1)} %get-tuple-element.16.q, bf16[2048,128]{1,0:T(8,128)(2,1)S(1)} %get-tuple-element.17.kc, bf16[2048,128]{1,0:T(8,128)(2,1)S(1)} %get-tuple-element.18.vc, bf16[2112,128]{1,0:T(8,128)(2,1)S(1)} %get-tuple-element.19.kn, ...), custom_call_target="tpu_custom_call" | custom-call | flops 9663676416 | bytes 2097152 | tf_op jit(solution)/shard_map/chunk_attention/pallas_call | solution.py:193
  227.6 1.3 pad_maximum_fusion.1
  228.9 66.5 %project.1 = (bf16[264,3072]{1,0:T(8,128)(2,1)}, bf16[264,3072]{1,0:T(8,128)(2,1)}) custom-call(bf16[8,264,384]{2,1,0:T(8,128)(2,1)} %bitcast.21, bf16[384,3072]{1,0:T(8,128)(2,1)} %w_o.1, bf16[264,3072]{1,0:T(8,128)(2,1)} %x.3, bf16[1,3072]{1,0:T(2,128)(2,1)} %reshape.47.g), custom_call_target="tpu_custom_call" | custom-call | flops 60000002048 | bytes 10000000 | tf_op jit(solution)/shard_map/project/pallas_call | solution.py:413
  295.5 111.6 %mlp.1 = bf16[264,3072]{1,0:T(8,128)(2,1)} custom-call(bf16[264,3072]{1,0:T(8,128)(2,1)} %get-tuple-element.23.hid, bf16[264,3072]{1,0:T(8,128)(2,1)} %get-tuple-element.24.mid, bf16[3072,1024]{1,0:T(8,128)(2,1)} %w_gate.1, bf16[3072,1024]{1,0:T(8,128)(2,1)} %w_up.1, bf16[1024,3072]{1,0:T(8,128)(2,1)} %w_down.1), custom_call_target="tpu_custom_call" | custom-call | flops 99999997952 | bytes 20000000 | tf_op jit(solution)/shard_map/mlp/pallas_call | solution.py:563
  407.2 1.0 copy-done.2
  408.2 1.0 copy-done.4
  409.2 0.9 copy-done.6
  410.1 0.7 copy-done.8
  410.8 0.7 copy-done.10
  411.5 8.6 %update_cache.1 = (bf16[4352,16,128]{2,1,0:T(8,128)(2,1)}, bf16[4352,16,128]{2,1,0:T(8,128)(2,1)}) custom-call(s32[65,256]{1,0:T(8,128)S(1)} %copy-done.6, s32[2112]{0:T(1024)S(1)} %copy-done.10, s32[2112]{0:T(1024)S(1)} %copy-done.8, bf16[2112,128]{1,0:T(8,128)(2,1)S(1)} %copy-done.2, ...), custom_call_target="tpu_custom_call", output_to_operand_aliasing={{0}: (5, {}), {1}: (6, {})} | custom-call | flops 4000000000 | bytes 1000000 | tf_op jit(solution)/shard_map/update_cache/pallas_call | solution.py:292
  420.1 1.2 copy.34
  (43 shorter events, 1.4 us)
Async XLA Ops:
  7.2 2.7 copy-start.12
  7.2 81.9 %all-gather.2.cloned.1.call-start = ((), (), s32[]{:S(2)}) async-start(), calls=%async_computation | async-start | bytes 14598144 | tf_op jit(solution)/shard_map/all_gather | solution.py:603
  9.9 1.8 copy-start.7
  9.9 1.8 copy-start.17
  16.2 1.7 copy-start.13
  16.2 1.8 copy-start.15
  16.2 2.1 copy-start.16
  18.2 2.1 copy-start.5
  18.2 2.1 copy-start.9
  89.1 2.1 copy-start
  104.2 37.7 %copy-start.1 = (bf16[2112,128]{1,0:T(8,128)(2,1)}, bf16[2112,128]{1,0:T(8,128)(2,1)S(1)}, u32[]{:S(2)}) copy-start(bf16[2112,128]{1,0:T(8,128)(2,1)S(1)} %get-tuple-element.19.kn) | copy-start | bytes 1622020
  104.2 37.7 %copy-start.3 = (bf16[2112,128]{1,0:T(8,128)(2,1)}, bf16[2112,128]{1,0:T(8,128)(2,1)S(1)}, u32[]{:S(2)}) copy-start(bf16[2112,128]{1,0:T(8,128)(2,1)S(1)} %get-tuple-element.20.vn) | copy-start | bytes 1622020
  114.8 5.8 %copy-start.11 = (bf16[64,1024,128]{2,1,0:T(8,128)(2,1)S(1)}, bf16[64,1024,128]{2,1,0:T(8,128)(2,1)}, u32[]{:S(2)}) copy-start(bf16[64,1024,128]{2,1,0:T(8,128)(2,1)} %get-tuple-element.21.kd) | copy-start | bytes 50331652
  407.1 1.0 copy-start.2
  408.2 1.0 copy-start.4
  409.2 0.9 copy-start.6
  410.1 0.7 copy-start.8
  410.8 0.7 copy-start.10
  411.5 8.6 %copy-start.14 = (bf16[264,3072]{1,0:T(8,128)(2,1)S(1)}, bf16[264,3072]{1,0:T(8,128)(2,1)}, u32[]{:S(2)}) copy-start(bf16[264,3072]{1,0:T(8,128)(2,1)} %mlp.1) | copy-start | bytes 4866052
Sparse Core Ops, SparseCore 0:
  11.8 67.7 all-gather.1

commit v2 on v0

v2 whole, which is shorter than its diff:
```python
import functools

import jax
import jax.numpy as jnp
from jax import lax
from jax.experimental import pallas as pl
from jax.experimental.pallas import tpu as pltpu
from jax.sharding import PartitionSpec as P

EPS = 1e-5
THETA = 500000.0
LOG2E = 1.4426950408889634
ANY = pl.BlockSpec(memory_space=pl.ANY)
SMEM = pl.BlockSpec(memory_space=pltpu.SMEM)
VMEM = pl.BlockSpec(memory_space=pltpu.VMEM)


def cost(flops, nbytes):
    return pl.CostEstimate(flops=int(flops), bytes_accessed=int(nbytes), transcendentals=0)


def ring_places(tp):
    chips = tp // 2
    me = lax.axis_index('tp')
    chip, core = me // 2, lax.rem(me, 2)
    sign = 1 - 2 * core
    peer = 2 * chip + 1 - core

    def chip_at(offset):
        return lax.rem(chip + sign * offset + 2 * chips, chips)

    return chip, core, peer, chip_at


def greet(*others):
    barrier = pltpu.get_barrier_semaphore()
    for other in others:
        pl.semaphore_signal(barrier, inc=1, device_id={'tp': other}, device_id_type=pl.DeviceIdType.MESH)
    pl.semaphore_wait(barrier, len(others))


def remote(src, dst, send, recv, to):
    return pltpu.make_async_remote_copy(src_ref=src, dst_ref=dst, send_sem=send, recv_sem=recv, device_id={'tp': to}, device_id_type=pl.DeviceIdType.MESH)


def front_kernel(tp, x, g, cos, sin, w_q, w_k, w_v, q_out, k_out, v_out,
                 hbuf, w, w_sem, ag_s, ag_r, pg_s, pg_r):
    chips = tp // 2
    chip, core, peer, chip_at = ring_places(tp)
    nxt = 2 * chip_at(1) + core
    prv = 2 * chip_at(-1) + core
    rows, d = x.shape
    n_q = q_out.shape[0]
    head = k_out.shape[2]
    halves = ((0, 144), (144, rows - 144))

    def gather(j, i):
        at = pl.ds(*halves[i])
        return remote(hbuf.at[j, at], hbuf.at[j + 1, at], ag_s.at[j, i], ag_r.at[j, i], nxt)

    def share(j):
        return remote(hbuf.at[j], hbuf.at[chips + j], pg_s.at[j], pg_r.at[j], peer)

    w_cols = n_q * head
    loads = [
        pltpu.make_async_copy(w_q, w.at[:, pl.ds(0, w_cols)], w_sem.at[0]),
        pltpu.make_async_copy(w_k, w.at[:, pl.ds(w_cols, head)], w_sem.at[1]),
        pltpu.make_async_copy(w_v, w.at[:, pl.ds(w_cols + head, head)], w_sem.at[2]),
    ]
    for load in loads:
        load.start()
    rows32 = x[...].astype(jnp.float32)
    inv_rms = lax.rsqrt(jnp.mean(rows32 * rows32, axis=-1, keepdims=True) + EPS)
    hbuf[0] = (rows32 * inv_rms * g[...].astype(jnp.float32)).astype(jnp.bfloat16)
    greet(peer, nxt, prv)
    for i in range(2):
        gather(0, i).start()
    share(0).start()

    def qkv(j, block):
        z = jnp.dot(hbuf[j], w[...], preferred_element_type=jnp.float32).astype(jnp.bfloat16)
        cs, sn = cos[block], sin[block]
        for n in range(n_q + 1):
            part = z[:, n * head:(n + 1) * head].astype(jnp.float32)
            val = (part * cs + pltpu.roll(part, head // 2, 1) * sn).astype(jnp.bfloat16)
            if n < n_q:
                q_out[n, block] = val
            else:
                k_out[block] = val
        v_out[block] = z[:, (n_q + 1) * head:]

    for load in loads:
        load.wait()
    qkv(0, 2 * chip + core)
    share(0).wait_recv()
    qkv(chips, peer)
    for j in range(1, chips):
        for i in range(2):
            gather(j - 1, i).wait_recv()
            if j < chips - 1:
                gather(j, i).start()
        share(j).start()
        qkv(j, 2 * chip_at(-j) + core)
        share(j).wait_recv()
        qkv(chips + j, 2 * chip_at(j) + 1 - core)
    for j in range(chips):
        share(j).wait_send()
        if j < chips - 1:
            for i in range(2):
                gather(j, i).wait_send()


def front(tp, x, g, cos, sin, w_q, w_k, w_v, head):
    rows, d = x.shape
    n_q = w_q.shape[1] // head
    chips = tp // 2
    bf = jnp.bfloat16
    dma = pltpu.SemaphoreType.DMA
    shape = lambda *dims: jax.ShapeDtypeStruct(dims, bf)
    new = shape(tp, rows, head)
    return pl.pallas_call(
        functools.partial(front_kernel, tp),
        out_shape=[shape(n_q, tp, rows, head), new, new],
        in_specs=[VMEM] * 4 + [ANY] * 3,
        out_specs=[VMEM] * 3,
        scratch_shapes=[
            pltpu.VMEM((2 * chips, rows, d), bf),
            pltpu.VMEM((d, (n_q + 2) * head), bf),
            dma((3,)), dma((chips - 1, 2)), dma((chips - 1, 2)), dma((chips,)), dma((chips,)),
        ],
        compiler_params=pltpu.CompilerParams(collective_id=0, has_side_effects=True, vmem_limit_bytes=60 * 2**20),
        cost_estimate=cost(6e10, 1e7),
        name="front",
    )(x, g.reshape(1, d), cos, sin, w_q, w_k, w_v)


def cache_kernel(parts, scale, pre_pages, dec_pages, table, reqs, pos, q, kn, vn, kp, vp, out, ko, vo, kc, vc,
                 kbuf, vbuf, prob, total, qf, of, in_sem, out_sem):
    n_q, n_dec, head = q.shape
    pool, page, _ = kbuf.shape
    step = pool // parts
    chunk_len = reqs.shape[0] - n_dec
    chunk_pages = chunk_len // page
    some = 16
    wide = some * page
    pairs = ((kp, kbuf, ko, kn, kc), (vp, vbuf, vo, vn, vc))

    def copy_in(c, i):
        at = pl.ds(i * step, step)
        return pltpu.make_async_copy(pairs[c][0].at[at], pairs[c][1].at[at], in_sem.at[c, i])

    def copy_out(c, i):
        at = pl.ds(i * step, step)
        return pltpu.make_async_copy(pairs[c][1].at[at], pairs[c][2].at[at], out_sem.at[c, i])

    for c in range(2):
        for i in range(parts):
            copy_in(c, i).start()
    qf[...] = q[...].astype(jnp.float32)
    req0 = reqs[0]

    def arrive(c):
        _, buf, _, new, line = pairs[c]
        for i in range(parts):
            copy_in(c, i).wait()

        def prefix(i, carry):
            line[pl.ds(pl.multiple_of(i * page, page), page), :] = buf[table[req0, i]]
            return carry

        lax.fori_loop(0, pre_pages, prefix, 0, unroll=8)

        def chunk(i, carry):
            rows = new[pl.ds(pl.multiple_of(i * page, page), page), :]
            buf[table[req0, pre_pages + i]] = rows
            line[pl.ds(pl.multiple_of((pre_pages + i) * page, page), page), :] = rows
            return carry

        lax.fori_loop(0, chunk_pages, chunk, 0, unroll=8)
        fresh = new[pl.ds(chunk_len, n_dec), :].astype(jnp.float32)
        of[c] = fresh

        def decode(i, carry):
            p = pos[chunk_len + i]
            at = table[reqs[chunk_len + i], p // page]
            hit = lax.broadcasted_iota(jnp.int32, (page, head), 0) == lax.rem(p, page)
            row = jnp.broadcast_to(of[c, pl.ds(i, 1), :], (page, head))
            buf[at] = jnp.where(hit, row, buf[at].astype(jnp.float32)).astype(jnp.bfloat16)
            return carry

        lax.fori_loop(0, n_dec, decode, 0, unroll=4)
        for i in range(parts):
            copy_out(c, i).start()

    def some_pages(buf, req, t):
        return jnp.concatenate([buf[table[req, t * some + j]] for j in range(some)], axis=0)

    col = lax.broadcasted_iota(jnp.int32, (8, dec_pages * page), 1)
    blank = jnp.zeros((8 - n_q, head), jnp.float32)
    both = 2

    arrive(0)

    def score(g, carry):
        for r in range(both):
            i = g * both + r
            req = reqs[chunk_len + i]
            qr = jnp.concatenate([qf[n, pl.ds(i, 1), :] for n in range(n_q)] + [blank], axis=0).astype(jnp.bfloat16)
            s = jnp.concatenate([
                lax.dot_general(qr, some_pages(kbuf, req, t), (((1,), (1,)), ((), ())), preferred_element_type=jnp.float32)
                for t in range(dec_pages // some)], axis=1)
            s = jnp.where(col <= pos[chunk_len + i], s, -1e30)
            p = jnp.exp2((s - jnp.max(s, axis=-1, keepdims=True)) * scale)
            total[i] = jnp.broadcast_to(jnp.sum(p, axis=-1, keepdims=True), (8, head))
            prob[i] = p
        return carry

    lax.fori_loop(0, n_dec // both, score, 0)
    arrive(1)

    def mix(g, carry):
        for r in range(both):
            i = g * both + r
            req = reqs[chunk_len + i]
            o = sum(
                jnp.dot(prob[i, :, t * wide:(t + 1) * wide].astype(jnp.bfloat16), some_pages(vbuf, req, t), preferred_element_type=jnp.float32)
                for t in range(dec_pages // some))
            o = o / total[i]
            for n in range(n_q):
                of[n, pl.ds(i, 1), :] = o[n:n + 1]
        return carry

    lax.fori_loop(0, n_dec // both, mix, 0)
    for n in range(n_q):
        out[:, n * head:(n + 1) * head] = of[n].astype(jnp.bfloat16)
    for c in range(2):
        for i in range(parts):
            copy_out(c, i).wait()


def cache_and_decode(table, reqs, pos, q, kn, vn, kp, vp, pre_pages, dec_pages):
    n_q, tokens, head = q.shape
    pool, page, _ = kp.shape
    n_dec = table.shape[0] - 1
    parts = 4
    bf, f32 = jnp.bfloat16, jnp.float32
    first = (tokens - n_dec) // n_dec
    full = jax.ShapeDtypeStruct(kp.shape, bf)
    line = jax.ShapeDtypeStruct((table.shape[1] * page, head), bf)
    dma = pltpu.SemaphoreType.DMA
    whole = lambda *dims: pl.BlockSpec(dims, lambda i: (0,) * len(dims))
    return pl.pallas_call(
        functools.partial(cache_kernel, parts, head ** -0.5 * LOG2E, pre_pages, dec_pages),
        grid=(1,),
        out_shape=[jax.ShapeDtypeStruct((n_dec, n_q * head), bf), full, full, line, line],
        in_specs=[SMEM, SMEM, SMEM, pl.BlockSpec((n_q, n_dec, head), lambda i: (0, first, 0)), whole(tokens, head), whole(tokens, head), ANY, ANY],
        out_specs=[whole(n_dec, n_q * head), ANY, ANY, whole(*line.shape), whole(*line.shape)],
        scratch_shapes=[
            pltpu.VMEM(kp.shape, bf), pltpu.VMEM(kp.shape, bf),
            pltpu.VMEM((n_dec, 8, dec_pages * page), f32), pltpu.VMEM((n_dec, 8, head), f32),
            pltpu.VMEM((n_q, n_dec, head), f32), pltpu.VMEM((n_q, n_dec, head), f32),
            dma((2, parts)), dma((2, parts)),
        ],
        compiler_params=pltpu.CompilerParams(vmem_limit_bytes=60 * 2**20),
        cost_estimate=cost(2e10, 1e8),
        name="cache_and_decode",
    )(table, reqs, pos, q, kn, vn, kp, vp)


def rope_tables(positions, head):
    half = head // 2
    lane = jnp.arange(head)
    inv_freq = THETA ** (-(lane % half).astype(jnp.float32) * 2.0 / head)
    angles = positions.astype(jnp.float32)[:, None] * inv_freq[None, :]
    return jnp.cos(angles), jnp.sin(angles) * jnp.where(lane < half, -1.0, 1.0)[None, :]


def attend_kernel(tp, parts, scale, tile, pre_len, q, dec, w_o, x, g, keys, vals, mid_out, hid_out,
                  score, top, weight, acc, o,
                  psend, precv, ssend, rrecv, ps_sem, pr_sem, ss_sem, rr_sem):
    chips = tp // 2
    chip, core, peer, chip_at = ring_places(tp)
    nxt = 2 * chip_at(1) + core
    prv = 2 * chip_at(-1) + core
    n_q, _, rows, head = q.shape
    wide = psend.shape[3]
    span = keys.shape[0]
    pre_tiles, all_tiles = pre_len // tile, span // tile
    n_dec = dec.shape[0]
    greet(peer, nxt, prv)

    def to_peer(s, p):
        return remote(psend.at[lax.rem(s, 2), p], precv.at[s, p], ps_sem.at[s, p], pr_sem.at[s, p], peer)

    def to_next(s, p):
        return remote(ssend.at[s, p], rrecv.at[s, p], ss_sem.at[s, p], rr_sem.at[s, p], nxt)

    def theirs(s):
        return 2 * chip_at(s + 1) + 1 - core

    def mine(s):
        return 2 * chip_at(-(s + 1)) + core

    def tiles(block):
        return jnp.minimum(pre_tiles + ((block + 1) * rows + tile - 1) // tile, all_tiles)

    def lanes(fn, v):
        out = v[:, :head]
        for i in range(1, tile // head):
            out = fn(out, v[:, i * head:(i + 1) * head])
        return out

    def at(t):
        return pl.ds(pl.multiple_of(t * tile, tile), tile)

    def scores(block, slot, t, masked):
        kt = keys[at(t), :]
        if masked:
            diff = lax.broadcasted_iota(jnp.int32, (rows, tile), 1) - lax.broadcasted_iota(jnp.int32, (rows, tile), 0)
            seen = diff <= pre_len + block * rows - t * tile
        for n in range(n_q):
            s = lax.dot_general(q[n, block], kt, (((1,), (1,)), ((), ())), preferred_element_type=jnp.float32)
            if masked:
                s = jnp.where(seen, s, -1e30)
            score[slot, n, :, at(t)] = s
            top[slot, n] = jnp.maximum(top[slot, n], lanes(jnp.maximum, s))

    def mix(slot, t):
        vt = vals[at(t), :]
        for n in range(n_q):
            p = jnp.exp2((score[slot, n, :, at(t)] - top[slot, n, :, :1]) * scale)
            weight[n] += lanes(jnp.add, p)
            acc[n] += jnp.dot(p.astype(jnp.bfloat16), vt, preferred_element_type=jnp.float32)

    def loop(lo, hi, fn):
        def body(t, carry):
            fn(t)
            return carry

        lax.fori_loop(lo, hi, body, 0)

    def run(slot, block, ahead, more):
        other = 1 - slot
        for n in range(n_q):
            top[slot, n] = jnp.broadcast_to(jnp.max(top[slot, n], axis=-1, keepdims=True), (rows, head))
        top[other] = jnp.full(top.shape[1:], -jnp.inf, jnp.float32)
        weight[...] = jnp.zeros_like(weight)
        acc[...] = jnp.zeros_like(acc)
        now = tiles(block)
        then = tiles(ahead) * more
        first = pre_tiles * more

        def both(masked):
            def fn(t):
                scores(ahead, other, t, masked)
                mix(slot, t)
            return fn

        loop(0, first, both(False))
        joint = jnp.maximum(first, jnp.minimum(now, then))
        loop(first, joint, both(True))
        loop(joint, then, lambda t: scores(ahead, other, t, True))
        loop(joint, now, lambda t: mix(slot, t))
        for n in range(n_q):
            total = jnp.sum(weight[n], axis=-1, keepdims=True)
            o[:, n * head:(n + 1) * head] = (acc[n] / total).astype(jnp.bfloat16)

        @pl.when(block == tp - 1)
        def _():
            o[pl.ds(rows - n_dec, n_dec), :] = dec[...]

    def product(p):
        cols = pl.ds(pl.multiple_of(p * wide, wide), wide)
        return jnp.dot(o[...], w_o[:, cols], preferred_element_type=jnp.float32)

    top[0] = jnp.full(top.shape[1:], -jnp.inf, jnp.float32)
    loop(0, tiles(theirs(0)), lambda t: scores(theirs(0), 0, t, True))

    def step(s, carry):
        run(0, theirs(s), mine(s), 1)

        def give(p):
            @pl.when(s > 1)
            def _():
                to_peer(s - 2, p).wait_send()

            psend[lax.rem(s, 2), p] = product(p).astype(jnp.bfloat16)
            to_peer(s, p).start()

        loop(0, parts, give)
        run(1, mine(s), theirs(s + 1), jnp.where(s < chips - 1, 1, 0))

        def take(p):
            own = product(p)
            to_peer(s, p).wait_recv()
            own = own + precv[s, p].astype(jnp.float32)
            cols = pl.ds(pl.multiple_of(p * wide, wide), wide)
            score[1, 0, :, cols] = own

            @pl.when(s > 0)
            def _():
                to_next(s - 1, p).wait_recv()
                score[1, 0, :, cols] = own + rrecv[s - 1, p].astype(jnp.float32)

            @pl.when(s < chips - 1)
            def _():
                ssend[s, p] = score[1, 0, :, cols].astype(jnp.bfloat16)
                to_next(s, p).start()

        loop(0, parts, take)
        return carry

    lax.fori_loop(0, chips, step, 0)

    total = score.at[1, 0]
    square = jnp.zeros((rows, 1), jnp.float32)
    for p in range(parts):
        cols = slice(p * wide, (p + 1) * wide)
        mid = (x[:, cols].astype(jnp.float32) + total[:, cols].astype(jnp.bfloat16).astype(jnp.float32)).astype(jnp.bfloat16)
        mid_out[:, cols] = mid
        mid = mid.astype(jnp.float32)
        total[:, cols] = mid
        square = square + jnp.sum(mid * mid, axis=-1, keepdims=True)
    inv_rms = lax.rsqrt(square / (parts * wide) + EPS)
    for p in range(parts):
        cols = slice(p * wide, (p + 1) * wide)
        hid_out[:, cols] = (total[:, cols] * inv_rms * g[:, cols].astype(jnp.float32)).astype(jnp.bfloat16)
    for p in range(parts):
        for s in range(chips):
            if s >= chips - 2:
                to_peer(s, p).wait_send()
            if s < chips - 1:
                to_next(s, p).wait_send()


def attend_project(tp, q, dec, w_o, x, g, keys, vals, pre_len):
    n_q, tokens, head = q.shape
    rows, d = x.shape
    n_dec = dec.shape[0]
    parts = 3
    wide = d // parts
    chips = tp // 2
    tile = 512
    span = keys.shape[0]
    bf, f32 = jnp.bfloat16, jnp.float32
    dma = pltpu.SemaphoreType.DMA
    block = lambda n: pltpu.VMEM((n, parts, rows, wide), bf)
    out = jax.ShapeDtypeStruct((rows, d), bf)
    return pl.pallas_call(
        functools.partial(attend_kernel, tp, parts, head ** -0.5 * LOG2E, tile, pre_len),
        out_shape=[out, out],
        in_specs=[VMEM] * 7,
        out_specs=[VMEM] * 2,
        scratch_shapes=[
            pltpu.VMEM((2, n_q, rows, span), f32), pltpu.VMEM((2, n_q, rows, head), f32),
            pltpu.VMEM((n_q, rows, head), f32), pltpu.VMEM((n_q, rows, head), f32),
            pltpu.VMEM((rows, n_q * head), bf),
            block(2), block(chips), block(chips - 1), block(chips - 1),
            dma((chips, parts)), dma((chips, parts)), dma((chips - 1, parts)), dma((chips - 1, parts)),
        ],
        compiler_params=pltpu.CompilerParams(collective_id=1, has_side_effects=True, vmem_limit_bytes=67043328),
        cost_estimate=cost(6e10, 1e7),
        name="attend_project",
    )(q.reshape(n_q, tp, rows, head), dec, w_o, x, g.reshape(1, d), keys, vals)


def mlp_kernel(tp, parts, hid, mid, w_gate, w_up, w_down, out,
               hbuf, gbuf, ubuf, dbuf, xbuf, act, acc, last, psend, precv, ssend, rrecv,
               in_sem, ag_s, ag_r, pg_s, pg_r, ps_sem, pr_sem, ss_sem, rr_sem):
    chips = tp // 2
    chip, core, peer, chip_at = ring_places(tp)
    nxt = 2 * chip_at(1) + core
    prv = 2 * chip_at(-1) + core
    _, rows, wide = acc.shape
    ff = gbuf.shape[1]
    tile = 256
    cut = 144
    halves = ((0, cut), (cut, rows - cut))
    loads = [pltpu.make_async_copy(a, b, in_sem.at[i]) for i, (a, b) in enumerate(
        ((hid, hbuf.at[0]), (w_gate, gbuf), (w_up, ubuf), (w_down, dbuf), (mid, xbuf)))]
    for load in loads:
        load.start()
    greet(peer, nxt, prv)

    def gather(j, i):
        first, n = halves[i]
        cut_rows = pl.ds(first, n)
        return remote(hbuf.at[j, cut_rows], hbuf.at[j + 1, cut_rows], ag_s.at[j, i], ag_r.at[j, i], nxt)

    def share(j):
        return remote(hbuf.at[j], hbuf.at[chips + j], pg_s.at[j], pg_r.at[j], peer)

    def to_peer(s, q):
        return remote(psend.at[s % 2, q], precv.at[s, q], ps_sem.at[s, q], pr_sem.at[s, q], peer)

    def to_next(s, q):
        return remote(ssend.at[s % 2, q], rrecv.at[s, q], ss_sem.at[s, q], rr_sem.at[s, q], nxt)

    def hidden_act(j):
        def body(t, carry):
            cols = pl.ds(pl.multiple_of(t * tile, tile), tile)
            gate = jnp.dot(hbuf[j], gbuf[:, cols], preferred_element_type=jnp.float32)
            up = jnp.dot(hbuf[j], ubuf[:, cols], preferred_element_type=jnp.float32)
            act[:, cols] = (gate * jax.nn.sigmoid(gate) * up).astype(jnp.bfloat16)
            return carry

        lax.fori_loop(0, ff // tile, body, 0)

    def down(q):
        cols = pl.ds(pl.multiple_of(q * wide, wide), wide)
        return jnp.dot(act[...], dbuf[:, cols], preferred_element_type=jnp.float32)

    def keep(j, dst):
        hidden_act(j)

        def body(q, carry):
            dst[q] = down(q)
            return carry

        lax.fori_loop(0, parts, body, 0)

    def give(j, s, before):
        hidden_act(j)

        def body(q, carry):
            if before is not None:
                to_peer(before, q).wait_send()
            psend[s % 2, q] = down(q).astype(jnp.bfloat16)
            to_peer(s, q).start()
            return carry

        lax.fori_loop(0, parts, body, 0)

    loads[0].wait()
    for i in range(2):
        gather(0, i).start()
    share(0).start()
    for load in loads[1:4]:
        load.wait()
    keep(0, last)
    share(0).wait_recv()
    end = chips - 1
    give(chips, end, None)
    for s in range(end):
        j = s + 1
        for i in range(2):
            gather(j - 1, i).wait_recv()
            if j < end:
                gather(j, i).start()
        share(j).start()
        keep(j, acc)
        share(j).wait_recv()
        give(chips + j, s, {0: None, 1: end, 2: 0}[s] if chips == 4 else None)

        def take(q, carry, s=s):
            to_peer(s, q).wait_recv()
            part = acc[q] + precv[s, q].astype(jnp.float32)
            if s > 0:
                to_next(s - 1, q).wait_recv()
                part = part + rrecv[s - 1, q].astype(jnp.float32)
            if s > 1:
                to_next(s - 2, q).wait_send()
            ssend[s % 2, q] = part.astype(jnp.bfloat16)
            to_next(s, q).start()
            return carry

        lax.fori_loop(0, parts, take, 0)

    loads[4].wait()
    for q in range(parts):
        cols = slice(q * wide, (q + 1) * wide)
        to_peer(end, q).wait_recv()
        part = last[q] + precv[end, q].astype(jnp.float32)
        to_next(end - 1, q).wait_recv()
        part = part + rrecv[end - 1, q].astype(jnp.float32)
        xbuf[:, cols] = (xbuf[:, cols].astype(jnp.float32) + part.astype(jnp.bfloat16).astype(jnp.float32)).astype(jnp.bfloat16)
    store = pltpu.make_async_copy(xbuf, out, in_sem.at[0])
    store.start()
    for j in range(chips):
        share(j).wait_send()
        if j < end:
            for i in range(2):
                gather(j, i).wait_send()
    for q in range(parts):
        to_peer(1, q).wait_send()
        to_peer(2, q).wait_send()
        for s in (end - 2, end - 1):
            to_next(s, q).wait_send()
    store.wait()


def mlp(tp, hid, mid, w_gate, w_up, w_down):
    rows, d = hid.shape
    ff = w_gate.shape[1]
    parts = 3
    wide = d // parts
    chips = tp // 2
    bf = jnp.bfloat16
    dma = pltpu.SemaphoreType.DMA
    block = lambda n: pltpu.VMEM((n, parts, rows, wide), bf)
    return pl.pallas_call(
        functools.partial(mlp_kernel, tp, parts),
        out_shape=jax.ShapeDtypeStruct((rows, d), bf),
        in_specs=[ANY] * 5,
        out_specs=ANY,
        scratch_shapes=[
            pltpu.VMEM((2 * chips, rows, d), bf),
            pltpu.VMEM((d, ff), bf), pltpu.VMEM((d, ff), bf), pltpu.VMEM((ff, d), bf),
            pltpu.VMEM((rows, d), bf), pltpu.VMEM((rows, ff), bf),
            pltpu.VMEM((parts, rows, wide), jnp.float32), pltpu.VMEM((parts, rows, wide), jnp.float32),
            block(2), block(chips), block(2), block(chips - 1),
            dma((5,)), dma((chips - 1, 2)), dma((chips - 1, 2)), dma((chips,)), dma((chips,)),
            dma((chips, parts)), dma((chips, parts)), dma((chips - 1, parts)), dma((chips - 1, parts)),
        ],
        compiler_params=pltpu.CompilerParams(collective_id=2, has_side_effects=True, vmem_limit_bytes=67043328),
        cost_estimate=cost(1e11, 2e7),
        name="mlp",
    )(hid, mid, w_gate, w_up, w_down)


def solution(mesh):
    tp = mesh.shape['tp']
    row_spec = P(('dp', 'tp'), None)
    group_vec = P('dp')
    table_spec = P('dp', None)
    cache_spec = P('dp', None, 'tp', None)
    col_split = P(None, 'tp')
    row_split = P('tp', None)
    gain_spec = P(None)

    def device_layer(x_in, req_ids, positions, block_table, ctx_len, k_pages, v_pages, w_q, w_k, w_v, w_o, w_gate, w_up, w_down, g_attn, g_mlp):
        pool, page, kv_heads, head = k_pages.shape
        tokens = positions.shape[0]
        n_dec = block_table.shape[0] - 1
        chunk_len = tokens - n_dec
        width = block_table.shape[1]
        pre_pages = width - chunk_len // page
        dec_pages = (pool - width) // n_dec
        n_q = w_q.shape[1] // head

        cos, sin = (t.reshape(tp, tokens // tp, head) for t in rope_tables(positions, head))
        q, kn, vn = front(tp, x_in, g_attn, cos, sin, w_q, w_k, w_v, head)
        q = q.reshape(n_q, tokens, head)
        kn, vn = kn.reshape(tokens, head), vn.reshape(tokens, head)
        dec, ko, vo, keys, vals = cache_and_decode(block_table, req_ids, positions, q, kn, vn, k_pages.reshape(pool, page, head), v_pages.reshape(pool, page, head), pre_pages, dec_pages)
        mid_rows, hidden_mlp = attend_project(tp, q, dec, w_o, x_in, g_mlp, keys, vals, pre_pages * page)
        x_out = mlp(tp, hidden_mlp, mid_rows, w_gate, w_up, w_down)
        return x_out, ko.reshape(k_pages.shape), vo.reshape(v_pages.shape)

    return jax.shard_map(device_layer, mesh=mesh, in_specs=(row_spec, group_vec, group_vec, table_spec, group_vec, cache_spec, cache_spec, col_split, col_split, col_split, row_split, col_split, col_split, row_split, gain_spec, gain_spec), out_specs=(row_spec, cache_spec, cache_spec), check_vma=False)
```

time: 956 us -> 310 us (0.32)
  local copies, waits for them, and re-layouts: 409 us -> 5.37 us
  Pallas kernels: 0 us -> 297 us
  matrix products: 227 us -> 0 us
  waiting for transfers between devices: 225 us -> 0 us
  other arithmetic: 74.1 us -> 6.34 us
  between operations: 16.5 us -> 0.68 us
    gather x7 -> x0, local copies, waits for them, and re-layouts: 309 us -> none  [the longest x1 132 us: attend(): v_cache[dec_rows].reshape(decode_len, key_span, kv_heads, head_dim)]
    pallas_call x0 -> x4, Pallas kernels: none -> 297 us  [the longest x1 113 us: mlp(): pl.pallas_call(functools.partial(mlp_kernel, tp, parts), out_shape=jax.Sh...]
    dot_general x11 -> x0, matrix products: 227 us -> none  [the longest x2 60.6 us: softmax_mix(): jnp.einsum(form, weights.astype(jnp.bfloat16), values, preferred_element_...]
    reduce_scatter x2 -> x0, waiting for transfers between devices: 141 us -> none  [the longest x1 70.7 us: device_layer(): lax.psum_scatter(down_part, 'tp', scatter_dimension=0, tiled=True)]
    unnamed x49 -> x1, local copies, waits for them, and re-layouts: 87.2 us -> 2.69 us
    all_gather x2 -> x0, waiting for transfers between devices: 83.7 us -> none  [the longest x1 64.7 us: device_layer(): lax.all_gather(rms_norm(mid_rows, g_mlp), 'tp', axis=0, tiled=True)]
    reduce_sum x4 -> x0, other arithmetic: 41.8 us -> none  [the longest x2 38.7 us: softmax_mix(): weight_sum = jnp.sum(weights, axis=-1, keepdims=True)]
    le x2 -> x0, other arithmetic: 11.1 us -> none  [the longest x1 10.2 us: attend(): key_pos[None, :] <= last_key[:chunk_len, None]]
  transfers between devices with their start and end apart: 4 -> 0, of which waited for: 4 -> 0; matrix products, arithmetic and copies ran while one was open for 5% -> 0% of each run, Pallas kernels for 0% -> 0%
where the time goes in v2:
time: 310 us; the launch traced here: 309 us
  Pallas kernels  297 us (96%)
  other arithmetic  6.34 us (2%)
  local copies, waits for them, and re-layouts  5.37 us (2%)
    pallas_call x1, Pallas kernels, mlp(): pl.pallas_call(functools.partial(mlp_kernel, tp, parts), out_shape=jax.Sh...  113 us
    pallas_call x1, Pallas kernels, attend_project(): pl.pallas_call(functools.partial(attend_kernel, tp, parts, head ** (-0.5)...  79.3 us
    pallas_call x1, Pallas kernels, front(): pl.pallas_call(functools.partial(front_kernel, tp), out_shape=[shape(n_q,...  66.8 us
    pallas_call x1, Pallas kernels, cache_and_decode(): pl.pallas_call(functools.partial(cache_kernel, parts, head ** (-0.5) * LO...  37.6 us

profile of v2, /device:TPU:112, one launch (start us, length us, event | category | flops | bytes accessed | tf_op | source)
XLA Modules:
  0.0 309.2 jit_solution(11474479459404090474)
XLA Ops:
  0.6 1.3 reshape.78.g
  1.9 1.3 reshape.84.g
  3.2 0.7 convert_element_type.10
  4.0 0.1 mul.29
  4.0 5.6 %fusion = (f32[8,264,128]{2,1,0:T(8,128)}, f32[8,264,128]{2,1,0:T(8,128)}) fusion(f32[128]{0:T(128)S(1)} %get-tuple-element.28, f32[128]{0:T(128)S(1)} %get-tuple-element.29, f32[8,264]{1,0:T(8,128)S(1)} %mul.29), kind=kLoop, calls=%fused_computation.2 | loop fusion | flops 540672 | bytes 2172160 | tf_op jit(solution)/shard_map/mul | solution.py:275
  9.7 66.8 %front.1 = (bf16[3,8,264,128]{3,2,1,0:T(8,128)(2,1)}, bf16[8,264,128]{2,1,0:T(8,128)(2,1)}, bf16[8,264,128]{2,1,0:T(8,128)(2,1)}) custom-call(bf16[264,3072]{1,0:T(8,128)(2,1)} %x.3, bf16[1,3072]{1,0:T(2,128)(2,1)} %reshape.78.g, f32[8,264,128]{2,1,0:T(8,128)} %get-tuple-element.27.cos, f32[8,264,128]{2,1,0:T(8,128)} %get-tuple-element.26.sin, ...), custom_call_target="tpu_custom_call" | custom-call | flops 60000002048 | bytes 10000000 | tf_op jit(solution)/shard_map/front/pallas_call | solution.py:121
  76.5 37.6 %cache_and_decode.1 = (bf16[64,384]{1,0:T(8,128)(2,1)}, bf16[4352,16,128]{2,1,0:T(8,128)(2,1)}, bf16[4352,16,128]{2,1,0:T(8,128)(2,1)}, bf16[4096,128]{1,0:T(8,128)(2,1)}, bf16[4096,128]{1,0:T(8,128)(2,1)}) custom-call(s32[65,256]{1,0:T(8,128)} %table.1, s32[2112]{0:T(1024)} %reqs.1, s32[2112]{0:T(1024)} %pos.1, bf16[3,2112,128]{2,1,0:T(8,128)(2,1)} %bitcast.15, ...), custom_call_target="tpu_custom_call" | custom-call | flops 20000000000 | bytes 100000000 | tf_op jit(solution)/shard_map/cache_and_decode/pallas_call | solution.py:252
  114.1 79.3 %attend_project.1 = (bf16[264,3072]{1,0:T(8,128)(2,1)}, bf16[264,3072]{1,0:T(8,128)(2,1)}) custom-call(bf16[3,8,264,128]{3,2,1,0:T(8,128)(2,1)} %get-tuple-element.13.q, bf16[64,384]{1,0:T(8,128)(2,1)} %get-tuple-element.16.dec, bf16[384,3072]{1,0:T(8,128)(2,1)} %w_o.1, bf16[264,3072]{1,0:T(8,128)(2,1)} %x.3, bf16[1,3072]{1,0:T(2,128)(2,1)} %reshape.84.g, ...), custom_call_target="tpu_custom_call" | custom-call | flops 60000002048 | bytes 10000000 | tf_op jit(solution)/shard_map/attend_project/pallas_call | solution.py:449
  193.3 113.2 %mlp.1 = bf16[264,3072]{1,0:T(8,128)(2,1)} custom-call(bf16[264,3072]{1,0:T(8,128)(2,1)} %get-tuple-element.19.hid, bf16[264,3072]{1,0:T(8,128)(2,1)} %get-tuple-element.20.mid, bf16[3072,1024]{1,0:T(8,128)(2,1)} %w_gate.1, bf16[3072,1024]{1,0:T(8,128)(2,1)} %w_up.1, bf16[1024,3072]{1,0:T(8,128)(2,1)} %w_down.1), custom_call_target="tpu_custom_call" | custom-call | flops 99999997952 | bytes 20000000 | tf_op jit(solution)/shard_map/mlp/pallas_call | solution.py:601
  306.5 2.7 copy.21
  (1 shorter events, 0.0 us)

commit v3 on v2

--- a/solution.py
+++ b/solution.py
@@ -2,6 +2,7 @@
 
 import jax
 import jax.numpy as jnp
+import numpy as np
 from jax import lax
 from jax.experimental import pallas as pl
 from jax.experimental.pallas import tpu as pltpu
@@ -43,8 +44,8 @@
     return pltpu.make_async_remote_copy(src_ref=src, dst_ref=dst, send_sem=send, recv_sem=recv, device_id={'tp': to}, device_id_type=pl.DeviceIdType.MESH)
 
 
-def front_kernel(tp, x, g, cos, sin, w_q, w_k, w_v, q_out, k_out, v_out,
-                 hbuf, w, w_sem, ag_s, ag_r, pg_s, pg_r):
+def front_kernel(tp, start, n_dec, pos, x, g, freq, w_q, w_k, w_v, q_out, k_out, v_out,
+                 hbuf, w, last_pos, w_sem, ag_s, ag_r, pg_s, pg_r):
     chips = tp // 2
     chip, core, peer, chip_at = ring_places(tp)
     nxt = 2 * chip_at(1) + core
@@ -58,8 +59,9 @@
         at = pl.ds(*halves[i])
         return remote(hbuf.at[j, at], hbuf.at[j + 1, at], ag_s.at[j, i], ag_r.at[j, i], nxt)
 
-    def share(j):
-        return remote(hbuf.at[j], hbuf.at[chips + j], pg_s.at[j], pg_r.at[j], peer)
+    def share(j, i):
+        at = pl.ds(*halves[i])
+        return remote(hbuf.at[j, at], hbuf.at[chips + j, at], pg_s.at[j, i], pg_r.at[j, i], peer)
 
     w_cols = n_q * head
     loads = [
@@ -71,46 +73,73 @@
         load.start()
     rows32 = x[...].astype(jnp.float32)
     inv_rms = lax.rsqrt(jnp.mean(rows32 * rows32, axis=-1, keepdims=True) + EPS)
-    hbuf[0] = (rows32 * inv_rms * g[...].astype(jnp.float32)).astype(jnp.bfloat16)
+    hbuf[0] = (rows32 * inv_rms * g[0:1, :]).astype(jnp.bfloat16)
     greet(peer, nxt, prv)
     for i in range(2):
         gather(0, i).start()
-    share(0).start()
-
-    def qkv(j, block):
-        z = jnp.dot(hbuf[j], w[...], preferred_element_type=jnp.float32).astype(jnp.bfloat16)
-        cs, sn = cos[block], sin[block]
-        for n in range(n_q + 1):
-            part = z[:, n * head:(n + 1) * head].astype(jnp.float32)
+    for i in range(2):
+        share(0, i).start()
+
+    def chunk_pos(block):
+        return (lax.broadcasted_iota(jnp.int32, (rows, head), 0) + (start + block * rows)).astype(jnp.float32)
+
+    last_pos[...] = chunk_pos(tp - 1)
+    first = pos.shape[0] - n_dec
+
+    def note(i, carry):
+        last_pos[pl.ds(rows - n_dec + i, 1), :] = jnp.full((1, head), pos[first + i], jnp.int32).astype(jnp.float32)
+        return carry
+
+    lax.fori_loop(0, n_dec, note, 0, unroll=8)
+    flip = jnp.where(lax.broadcasted_iota(jnp.int32, (1, head), 1) < head // 2, -1.0, 1.0)
+
+    def qkv(j, block, i):
+        lo, n = halves[i]
+        at = pl.ds(lo, n)
+        z = jnp.dot(hbuf[j, at, :], w[...], preferred_element_type=jnp.float32).astype(jnp.bfloat16)
+        is_last = jnp.broadcast_to(block, (n, head)) == tp - 1
+        angle = jnp.where(is_last, last_pos[at, :], chunk_pos(block)[lo:lo + n]) * freq[...]
+        cs, sn = jnp.cos(angle), jnp.sin(angle) * flip
+        for m in range(n_q + 1):
+            part = z[:, m * head:(m + 1) * head].astype(jnp.float32)
             val = (part * cs + pltpu.roll(part, head // 2, 1) * sn).astype(jnp.bfloat16)
-            if n < n_q:
-                q_out[n, block] = val
+            if m < n_q:
+                q_out[m, block, at, :] = val
             else:
-                k_out[block] = val
-        v_out[block] = z[:, (n_q + 1) * head:]
+                k_out[block, at, :] = val
+        v_out[block, at, :] = z[:, (n_q + 1) * head:]
 
     for load in loads:
         load.wait()
-    qkv(0, 2 * chip + core)
-    share(0).wait_recv()
-    qkv(chips, peer)
-    for j in range(1, chips):
+    for i in range(2):
+        qkv(0, 2 * chip + core, i)
+    for i in range(2):
+        share(0, i).wait_recv()
+        qkv(chips, peer, i)
+
+    def hop(j, carry):
         for i in range(2):
             gather(j - 1, i).wait_recv()
+
+            @pl.when(j < chips - 1)
+            def _():
+                gather(j, i).start()
+
+            share(j, i).start()
+            qkv(j, 2 * chip_at(-j) + core, i)
+            share(j, i).wait_recv()
+            qkv(chips + j, 2 * chip_at(j) + 1 - core, i)
+        return carry
+
+    lax.fori_loop(1, chips, hop, 0)
+    for j in range(chips):
+        for i in range(2):
+            share(j, i).wait_send()
             if j < chips - 1:
-                gather(j, i).start()
-        share(j).start()
-        qkv(j, 2 * chip_at(-j) + core)
-        share(j).wait_recv()
-        qkv(chips + j, 2 * chip_at(j) + 1 - core)
-    for j in range(chips):
-        share(j).wait_send()
-        if j < chips - 1:
-            for i in range(2):
                 gather(j, i).wait_send()
 
 
-def front(tp, x, g, cos, sin, w_q, w_k, w_v, head):
+def front(tp, pos, x, g, w_q, w_k, w_v, head, n_dec, start):
     rows, d = x.shape
     n_q = w_q.shape[1] // head
     chips = tp // 2
@@ -118,25 +147,90 @@
     dma = pltpu.SemaphoreType.DMA
     shape = lambda *dims: jax.ShapeDtypeStruct(dims, bf)
     new = shape(tp, rows, head)
+    freq = (THETA ** (-(np.arange(head) % (head // 2)) * 2.0 / head)).astype(np.float32)[None, :]
     return pl.pallas_call(
-        functools.partial(front_kernel, tp),
+        functools.partial(front_kernel, tp, start, n_dec),
         out_shape=[shape(n_q, tp, rows, head), new, new],
-        in_specs=[VMEM] * 4 + [ANY] * 3,
+        in_specs=[SMEM] + [VMEM] * 3 + [ANY] * 3,
         out_specs=[VMEM] * 3,
         scratch_shapes=[
             pltpu.VMEM((2 * chips, rows, d), bf),
             pltpu.VMEM((d, (n_q + 2) * head), bf),
-            dma((3,)), dma((chips - 1, 2)), dma((chips - 1, 2)), dma((chips,)), dma((chips,)),
+            pltpu.VMEM((rows, head), jnp.float32),
+            dma((3,)), dma((chips - 1, 2)), dma((chips - 1, 2)), dma((chips, 2)), dma((chips, 2)),
         ],
         compiler_params=pltpu.CompilerParams(collective_id=0, has_side_effects=True, vmem_limit_bytes=60 * 2**20),
         cost_estimate=cost(6e10, 1e7),
         name="front",
-    )(x, g.reshape(1, d), cos, sin, w_q, w_k, w_v)
-
-
-def cache_kernel(parts, scale, pre_pages, dec_pages, table, reqs, pos, q, kn, vn, kp, vp, out, ko, vo, kc, vc,
-                 kbuf, vbuf, prob, total, qf, of, in_sem, out_sem):
-    n_q, n_dec, head = q.shape
+    )(pos, x, g, jnp.asarray(freq), w_q, w_k, w_v)
+
+
+def lanes(fn, v, head):
+    out = v[:, :head]
+    for i in range(1, v.shape[1] // head):
+        out = fn(out, v[:, i * head:(i + 1) * head])
+    return out
+
+
+def tile_at(t, tile):
+    return pl.ds(pl.multiple_of(t * tile, tile), tile)
+
+
+def tile_count(block, rows, pre_len, span, tile):
+    return jnp.minimum(pre_len // tile + ((block + 1) * rows + tile - 1) // tile, span // tile)
+
+
+def tile_scores(q, keys, score, top, block, t, tile, pre_len, masked):
+    n_q, _, rows, head = q.shape
+    kt = keys[tile_at(t, tile), :]
+    if masked:
+        diff = lax.broadcasted_iota(jnp.int32, (rows, tile), 1) - lax.broadcasted_iota(jnp.int32, (rows, tile), 0)
+        seen = diff <= pre_len + block * rows - t * tile
+    for n in range(n_q):
+        s = lax.dot_general(q[n, block], kt, (((1,), (1,)), ((), ())), preferred_element_type=jnp.float32)
+        if masked:
+            s = jnp.where(seen, s, -1e30)
+        score[n, :, tile_at(t, tile)] = s
+        top[n] = jnp.maximum(top[n], lanes(jnp.maximum, s, head))
+
+
+def tile_mix(vals, score, top, weight, acc, t, tile, scale):
+    n_q, _, head = acc.shape
+    vt = vals[tile_at(t, tile), :]
+    for n in range(n_q):
+        p = jnp.exp2((score[n, :, tile_at(t, tile)] - top[n, :, :1]) * scale)
+        weight[n] += lanes(jnp.add, p, head)
+        acc[n] += jnp.dot(p.astype(jnp.bfloat16), vt, preferred_element_type=jnp.float32)
+
+
+def open_mix(top, weight, acc):
+    for n in range(top.shape[0]):
+        top[n] = jnp.broadcast_to(jnp.max(top[n], axis=-1, keepdims=True), top.shape[1:])
+    weight[...] = jnp.zeros_like(weight)
+    acc[...] = jnp.zeros_like(acc)
+
+
+def close_mix(weight, acc, o):
+    n_q, _, head = acc.shape
+    for n in range(n_q):
+        total = jnp.sum(weight[n], axis=-1, keepdims=True)
+        o[:, n * head:(n + 1) * head] = (acc[n] / total).astype(jnp.bfloat16)
+
+
+def loop(lo, hi, fn):
+    def body(t, carry):
+        fn(t)
+        return carry
+
+    lax.fori_loop(lo, hi, body, 0)
+
+
+def cache_kernel(tp, tile, parts, scale, pre_pages, dec_pages, table, reqs, pos, q, kn, vn, kp, vp, out, ko, vo, kc, vc, early,
+                 kbuf, vbuf, prob, total, qf, of, score_buf, top, weight, acc, in_sem, out_sem):
+    n_q, n_dec, head = qf.shape
+    rows = q.shape[2]
+    chip, core, peer, chip_at = ring_places(tp)
+    ahead = (2 * chip_at(1) + 1 - core, 2 * chip_at(-1) + core)
     pool, page, _ = kbuf.shape
     step = pool // parts
     chunk_len = reqs.shape[0] - n_dec
@@ -156,7 +250,7 @@
     for c in range(2):
         for i in range(parts):
             copy_in(c, i).start()
-    qf[...] = q[...].astype(jnp.float32)
+    qf[...] = q[:, tp - 1, pl.ds(rows - n_dec, n_dec), :].astype(jnp.float32)
     req0 = reqs[0]
 
     def arrive(c):
@@ -197,7 +291,7 @@
 
     col = lax.broadcasted_iota(jnp.int32, (8, dec_pages * page), 1)
     blank = jnp.zeros((8 - n_q, head), jnp.float32)
-    both = 2
+    both = 8
 
     arrive(0)
 
@@ -216,6 +310,21 @@
         return carry
 
     lax.fori_loop(0, n_dec // both, score, 0)
+    pre_len = pre_pages * page
+    span = kc.shape[0]
+
+    def block_scores(block):
+        top[...] = jnp.full(top.shape, -jnp.inf, jnp.float32)
+        loop(0, tile_count(block, rows, pre_len, span, tile),
+             lambda t: tile_scores(q, kc, score_buf, top, block, t, tile, pre_len, True))
+
+    def block_mix(block, e):
+        open_mix(top, weight, acc)
+        loop(0, tile_count(block, rows, pre_len, span, tile),
+             lambda t: tile_mix(vc, score_buf, top, weight, acc, t, tile, scale))
+        close_mix(weight, acc, early.at[e])
+
+    block_scores(ahead[0])
     arrive(1)
 
     def mix(g, carry):
@@ -233,50 +342,46 @@
     lax.fori_loop(0, n_dec // both, mix, 0)
     for n in range(n_q):
         out[:, n * head:(n + 1) * head] = of[n].astype(jnp.bfloat16)
+    block_mix(ahead[0], 0)
+    block_scores(ahead[1])
+    block_mix(ahead[1], 1)
     for c in range(2):
         for i in range(parts):
             copy_out(c, i).wait()
 
 
-def cache_and_decode(table, reqs, pos, q, kn, vn, kp, vp, pre_pages, dec_pages):
-    n_q, tokens, head = q.shape
+def cache_and_decode(tp, table, reqs, pos, q, kn, vn, kp, vp, pre_pages, dec_pages, tile):
+    n_q, _, rows, head = q.shape
+    tokens = tp * rows
     pool, page, _ = kp.shape
     n_dec = table.shape[0] - 1
     parts = 4
     bf, f32 = jnp.bfloat16, jnp.float32
-    first = (tokens - n_dec) // n_dec
     full = jax.ShapeDtypeStruct(kp.shape, bf)
     line = jax.ShapeDtypeStruct((table.shape[1] * page, head), bf)
+    early = jax.ShapeDtypeStruct((2, rows, n_q * head), bf)
     dma = pltpu.SemaphoreType.DMA
-    whole = lambda *dims: pl.BlockSpec(dims, lambda i: (0,) * len(dims))
     return pl.pallas_call(
-        functools.partial(cache_kernel, parts, head ** -0.5 * LOG2E, pre_pages, dec_pages),
-        grid=(1,),
-        out_shape=[jax.ShapeDtypeStruct((n_dec, n_q * head), bf), full, full, line, line],
-        in_specs=[SMEM, SMEM, SMEM, pl.BlockSpec((n_q, n_dec, head), lambda i: (0, first, 0)), whole(tokens, head), whole(tokens, head), ANY, ANY],
-        out_specs=[whole(n_dec, n_q * head), ANY, ANY, whole(*line.shape), whole(*line.shape)],
+        functools.partial(cache_kernel, tp, tile, parts, head ** -0.5 * LOG2E, pre_pages, dec_pages),
+        out_shape=[jax.ShapeDtypeStruct((n_dec, n_q * head), bf), full, full, line, line, early],
+        in_specs=[SMEM] * 3 + [VMEM] * 3 + [ANY] * 2,
+        out_specs=[VMEM, ANY, ANY, VMEM, VMEM, VMEM],
         scratch_shapes=[
             pltpu.VMEM(kp.shape, bf), pltpu.VMEM(kp.shape, bf),
             pltpu.VMEM((n_dec, 8, dec_pages * page), f32), pltpu.VMEM((n_dec, 8, head), f32),
             pltpu.VMEM((n_q, n_dec, head), f32), pltpu.VMEM((n_q, n_dec, head), f32),
+            pltpu.VMEM((n_q, rows, line.shape[0]), f32), pltpu.VMEM((n_q, rows, head), f32),
+            pltpu.VMEM((n_q, rows, head), f32), pltpu.VMEM((n_q, rows, head), f32),
             dma((2, parts)), dma((2, parts)),
         ],
-        compiler_params=pltpu.CompilerParams(vmem_limit_bytes=60 * 2**20),
-        cost_estimate=cost(2e10, 1e8),
+        compiler_params=pltpu.CompilerParams(vmem_limit_bytes=67043328),
+        cost_estimate=cost(4e10, 1e8),
         name="cache_and_decode",
     )(table, reqs, pos, q, kn, vn, kp, vp)
 
 
-def rope_tables(positions, head):
-    half = head // 2
-    lane = jnp.arange(head)
-    inv_freq = THETA ** (-(lane % half).astype(jnp.float32) * 2.0 / head)
-    angles = positions.astype(jnp.float32)[:, None] * inv_freq[None, :]
-    return jnp.cos(angles), jnp.sin(angles) * jnp.where(lane < half, -1.0, 1.0)[None, :]
-
-
-def attend_kernel(tp, parts, scale, tile, pre_len, q, dec, w_o, x, g, keys, vals, mid_out, hid_out,
-                  score, top, weight, acc, o,
+def attend_kernel(tp, parts, scale, tile, pre_len, q, dec, early, w_o_any, x_any, g, keys, vals, mid_out, hid_out,
+                  w_o, x, in_sem, score, top, weight, acc, o,
                   psend, precv, ssend, rrecv, ps_sem, pr_sem, ss_sem, rr_sem):
     chips = tp // 2
     chip, core, peer, chip_at = ring_places(tp)
@@ -287,6 +392,9 @@
     span = keys.shape[0]
     pre_tiles, all_tiles = pre_len // tile, span // tile
     n_dec = dec.shape[0]
+    loads = [pltpu.make_async_copy(w_o_any, w_o, in_sem.at[0]), pltpu.make_async_copy(x_any, x, in_sem.at[1])]
+    for load in loads:
+        load.start()
     greet(peer, nxt, prv)
 
     def to_peer(s, p):
@@ -302,53 +410,26 @@
         return 2 * chip_at(-(s + 1)) + core
 
     def tiles(block):
-        return jnp.minimum(pre_tiles + ((block + 1) * rows + tile - 1) // tile, all_tiles)
-
-    def lanes(fn, v):
-        out = v[:, :head]
-        for i in range(1, tile // head):
-            out = fn(out, v[:, i * head:(i + 1) * head])
-        return out
-
-    def at(t):
-        return pl.ds(pl.multiple_of(t * tile, tile), tile)
+        return tile_count(block, rows, pre_len, span, tile)
 
     def scores(block, slot, t, masked):
-        kt = keys[at(t), :]
-        if masked:
-            diff = lax.broadcasted_iota(jnp.int32, (rows, tile), 1) - lax.broadcasted_iota(jnp.int32, (rows, tile), 0)
-            seen = diff <= pre_len + block * rows - t * tile
-        for n in range(n_q):
-            s = lax.dot_general(q[n, block], kt, (((1,), (1,)), ((), ())), preferred_element_type=jnp.float32)
-            if masked:
-                s = jnp.where(seen, s, -1e30)
-            score[slot, n, :, at(t)] = s
-            top[slot, n] = jnp.maximum(top[slot, n], lanes(jnp.maximum, s))
+        tile_scores(q, keys, score.at[slot], top.at[slot], block, t, tile, pre_len, masked)
 
     def mix(slot, t):
-        vt = vals[at(t), :]
-        for n in range(n_q):
-            p = jnp.exp2((score[slot, n, :, at(t)] - top[slot, n, :, :1]) * scale)
-            weight[n] += lanes(jnp.add, p)
-            acc[n] += jnp.dot(p.astype(jnp.bfloat16), vt, preferred_element_type=jnp.float32)
-
-    def loop(lo, hi, fn):
-        def body(t, carry):
-            fn(t)
-            return carry
-
-        lax.fori_loop(lo, hi, body, 0)
+        tile_mix(vals, score.at[slot], top.at[slot], weight, acc, t, tile, scale)
+
+    def finish(block):
+        @pl.when(block == tp - 1)
+        def _():
+            o[pl.ds(rows - n_dec, n_dec), :] = dec[...]
 
     def run(slot, block, ahead, more):
         other = 1 - slot
-        for n in range(n_q):
-            top[slot, n] = jnp.broadcast_to(jnp.max(top[slot, n], axis=-1, keepdims=True), (rows, head))
+        open_mix(top.at[slot], weight, acc)
         top[other] = jnp.full(top.shape[1:], -jnp.inf, jnp.float32)
-        weight[...] = jnp.zeros_like(weight)
-        acc[...] = jnp.zeros_like(acc)
         now = tiles(block)
         then = tiles(ahead) * more
-        first = pre_tiles * more
+        first = pre_len // tile * more
 
         def both(masked):
             def fn(t):
@@ -361,24 +442,14 @@
         loop(first, joint, both(True))
         loop(joint, then, lambda t: scores(ahead, other, t, True))
         loop(joint, now, lambda t: mix(slot, t))
-        for n in range(n_q):
-            total = jnp.sum(weight[n], axis=-1, keepdims=True)
-            o[:, n * head:(n + 1) * head] = (acc[n] / total).astype(jnp.bfloat16)
-
-        @pl.when(block == tp - 1)
-        def _():
-            o[pl.ds(rows - n_dec, n_dec), :] = dec[...]
+        close_mix(weight, acc, o)
+        finish(block)
 
     def product(p):
         cols = pl.ds(pl.multiple_of(p * wide, wide), wide)
         return jnp.dot(o[...], w_o[:, cols], preferred_element_type=jnp.float32)
 
-    top[0] = jnp.full(top.shape[1:], -jnp.inf, jnp.float32)
-    loop(0, tiles(theirs(0)), lambda t: scores(theirs(0), 0, t, True))
-
-    def step(s, carry):
-        run(0, theirs(s), mine(s), 1)
-
+    def give_all(s):
         def give(p):
             @pl.when(s > 1)
             def _():
@@ -388,8 +459,8 @@
             to_peer(s, p).start()
 
         loop(0, parts, give)
-        run(1, mine(s), theirs(s + 1), jnp.where(s < chips - 1, 1, 0))
-
+
+    def take_all(s):
         def take(p):
             own = product(p)
             to_peer(s, p).wait_recv()
@@ -408,8 +479,39 @@
                 to_next(s, p).start()
 
         loop(0, parts, take)
+
+    def step(s, carry):
+        @pl.when(s == 0)
+        def _():
+            o[...] = early[0]
+            finish(theirs(0))
+
+        @pl.when(s > 0)
+        def _():
+            run(0, theirs(s), mine(s), 1)
+
+        give_all(s)
+
+        @pl.when(s == 0)
+        def _():
+            o[...] = early[1]
+            finish(mine(0))
+
+        @pl.when(s > 0)
+        def _():
+            run(1, mine(s), theirs(s + 1), jnp.where(s < chips - 1, 1, 0))
+
+        take_all(s)
+
+        @pl.when(s == 0)
+        def _():
+            top[0] = jnp.full(top.shape[1:], -jnp.inf, jnp.float32)
+            loop(0, tiles(theirs(1)), lambda t: scores(theirs(1), 0, t, True))
+
         return carry
 
+    for load in loads:
+        load.wait()
     lax.fori_loop(0, chips, step, 0)
 
     total = score.at[1, 0]
@@ -424,7 +526,7 @@
     inv_rms = lax.rsqrt(square / (parts * wide) + EPS)
     for p in range(parts):
         cols = slice(p * wide, (p + 1) * wide)
-        hid_out[:, cols] = (total[:, cols] * inv_rms * g[:, cols].astype(jnp.float32)).astype(jnp.bfloat16)
+        hid_out[:, cols] = (total[:, cols] * inv_rms * g[1:2, cols]).astype(jnp.bfloat16)
     for p in range(parts):
         for s in range(chips):
             if s >= chips - 2:
@@ -433,14 +535,12 @@
                 to_next(s, p).wait_send()
 
 
-def attend_project(tp, q, dec, w_o, x, g, keys, vals, pre_len):
-    n_q, tokens, head = q.shape
-    rows, d = x.shape
-    n_dec = dec.shape[0]
+def attend_project(tp, q, dec, early, w_o, x, g, keys, vals, pre_len, tile):
+    n_q, _, rows, head = q.shape
+    d = x.shape[1]
     parts = 3
     wide = d // parts
     chips = tp // 2
-    tile = 512
     span = keys.shape[0]
     bf, f32 = jnp.bfloat16, jnp.float32
     dma = pltpu.SemaphoreType.DMA
@@ -449,9 +549,10 @@
     return pl.pallas_call(
         functools.partial(attend_kernel, tp, parts, head ** -0.5 * LOG2E, tile, pre_len),
         out_shape=[out, out],
-        in_specs=[VMEM] * 7,
+        in_specs=[VMEM] * 3 + [ANY] * 2 + [VMEM] * 3,
         out_specs=[VMEM] * 2,
         scratch_shapes=[
+            pltpu.VMEM(w_o.shape, bf), pltpu.VMEM((rows, d), bf), dma((2,)),
             pltpu.VMEM((2, n_q, rows, span), f32), pltpu.VMEM((2, n_q, rows, head), f32),
             pltpu.VMEM((n_q, rows, head), f32), pltpu.VMEM((n_q, rows, head), f32),
             pltpu.VMEM((rows, n_q * head), bf),
@@ -461,7 +562,7 @@
         compiler_params=pltpu.CompilerParams(collective_id=1, has_side_effects=True, vmem_limit_bytes=67043328),
         cost_estimate=cost(6e10, 1e7),
         name="attend_project",
-    )(q.reshape(n_q, tp, rows, head), dec, w_o, x, g.reshape(1, d), keys, vals)
+    )(q, dec, early, w_o, x, g, keys, vals)
 
 
 def mlp_kernel(tp, parts, hid, mid, w_gate, w_up, w_down, out,
@@ -638,12 +739,12 @@
         dec_pages = (pool - width) // n_dec
         n_q = w_q.shape[1] // head
 
-        cos, sin = (t.reshape(tp, tokens // tp, head) for t in rope_tables(positions, head))
-        q, kn, vn = front(tp, x_in, g_attn, cos, sin, w_q, w_k, w_v, head)
-        q = q.reshape(n_q, tokens, head)
+        gains = jnp.stack([g_attn, g_mlp]).astype(jnp.float32)
+        q, kn, vn = front(tp, positions, x_in, gains, w_q, w_k, w_v, head, n_dec, pre_pages * page)
         kn, vn = kn.reshape(tokens, head), vn.reshape(tokens, head)
-        dec, ko, vo, keys, vals = cache_and_decode(block_table, req_ids, positions, q, kn, vn, k_pages.reshape(pool, page, head), v_pages.reshape(pool, page, head), pre_pages, dec_pages)
-        mid_rows, hidden_mlp = attend_project(tp, q, dec, w_o, x_in, g_mlp, keys, vals, pre_pages * page)
+        tile = 512
+        dec, ko, vo, keys, vals, early = cache_and_decode(tp, block_table, req_ids, positions, q, kn, vn, k_pages.reshape(pool, page, head), v_pages.reshape(pool, page, head), pre_pages, dec_pages, tile)
+        mid_rows, hidden_mlp = attend_project(tp, q, dec, early, w_o, x_in, gains, keys, vals, pre_pages * page, tile)
         x_out = mlp(tp, hidden_mlp, mid_rows, w_gate, w_up, w_down)
         return x_out, ko.reshape(k_pages.shape), vo.reshape(v_pages.shape)
 

time: 310 us -> 292 us (0.942)
  Pallas kernels: 297 us -> 286 us
  other arithmetic: 6.34 us -> 0.63 us
    pallas_call x1, Pallas kernels: 79.3 us -> 66.7 us  [attend_project(): pl.pallas_call(functools.partial(attend_kernel, tp, parts, head ** (-0.5)...]
    mul x1 -> x0, other arithmetic: 5.63 us -> none  [rope_tables(): jnp.sin(angles) * jnp.where(lane < half, -1.0, 1.0)[None, :]]
    pallas_call x2, Pallas kernels: 104 us -> 108 us  [the longest x1 64.3 us: front(): pl.pallas_call(functools.partial(front_kernel, tp, start, n_dec), out_sha...]
where the time goes in v3:
time: 292 us
  Pallas kernels  286 us (98%)
  local copies, waits for them, and re-layouts  4.09 us (1%)
    pallas_call x1, Pallas kernels, mlp(): pl.pallas_call(functools.partial(mlp_kernel, tp, parts), out_shape=jax.Sh...  112 us
    pallas_call x1, Pallas kernels, attend_project(): pl.pallas_call(functools.partial(attend_kernel, tp, parts, head ** (-0.5)...  66.7 us
    pallas_call x1, Pallas kernels, front(): pl.pallas_call(functools.partial(front_kernel, tp, start, n_dec), out_sha...  64.3 us
    pallas_call x1, Pallas kernels, cache_and_decode(): pl.pallas_call(functools.partial(cache_kernel, tp, tile, parts, head ** (...  43.7 us

profile of v3, /device:TPU:112, one launch (start us, length us, event | category | flops | bytes accessed | tf_op | source)
XLA Modules:
  0.0 291.6 jit_solution(10712114838828101362)
XLA Ops:
  0.6 0.7 stack.9
  1.3 0.7 stack.10
  2.0 0.6 maximum_convert_fusion.g
  2.7 64.3 %front.1 = (bf16[3,8,264,128]{3,2,1,0:T(8,128)(2,1)}, bf16[8,264,128]{2,1,0:T(8,128)(2,1)}, bf16[8,264,128]{2,1,0:T(8,128)(2,1)}) custom-call(s32[2112]{0:T(1024)} %pos.3, bf16[264,3072]{1,0:T(8,128)(2,1)} %x_any.1, f32[2,3072]{1,0:T(2,128)} %maximum_convert_fusion.g, f32[1,128]{1,0:T(1,128)} %constant.2.clone.freq, bf16[3072,384]{1,0:T(8,128)(2,1)} %w_q.1, ...), custom_call_target="tpu_custom_call" | custom-call | flops 60000002048 | bytes 10000000 | tf_op jit(solution)/shard_map/front/pallas_call | solution.py:151
  66.9 43.7 %cache_and_decode.1 = (bf16[64,384]{1,0:T(8,128)(2,1)}, bf16[4352,16,128]{2,1,0:T(8,128)(2,1)}, bf16[4352,16,128]{2,1,0:T(8,128)(2,1)}, bf16[4096,128]{1,0:T(8,1...) custom-call(s32[65,256]{1,0:T(8,128)} %table.1, s32[2112]{0:T(1024)} %reqs.1, s32[2112]{0:T(1024)} %pos.3, ...), custom_call_target="tpu_custom_call" | custom-call | flops 40000000000 | bytes 100000000 | tf_op jit(solution)/shard_map/cache_and_decode/pallas_call | solution.py:364
  110.6 66.7 %attend_project.1 = (bf16[264,3072]{1,0:T(8,128)(2,1)}, bf16[264,3072]{1,0:T(8,128)(2,1)}) custom-call(bf16[3,8,264,128]{3,2,1,0:T(8,128)(2,1)} %get-tuple-element.14.q, bf16[64,384]{1,0:T(8,128)(2,1)} %get-tuple-element.17.dec, bf16[2,264,384]{2,1,0:T(8,128)(2,1)} %get-tuple-element.18.early, bf16[384,3072]{1,0:T(8,128)(2,1)} %w_o_any.1, ...), custom_call_target="tpu_custom_call" | custom-call | flops 60000002048 | bytes 10000000 | tf_op jit(solution)/shard_map/attend_project/pallas_call | solution.py:549
  177.3 111.6 %mlp.1 = bf16[264,3072]{1,0:T(8,128)(2,1)} custom-call(bf16[264,3072]{1,0:T(8,128)(2,1)} %get-tuple-element.21.hid, bf16[264,3072]{1,0:T(8,128)(2,1)} %get-tuple-element.22.mid, bf16[3072,1024]{1,0:T(8,128)(2,1)} %w_gate.1, bf16[3072,1024]{1,0:T(8,128)(2,1)} %w_up.1, bf16[1024,3072]{1,0:T(8,128)(2,1)} %w_down.1), custom_call_target="tpu_custom_call" | custom-call | flops 99999997952 | bytes 20000000 | tf_op jit(solution)/shard_map/mlp/pallas_call | solution.py:702
  288.9 2.7 copy.22

commit v4 on v3

--- a/solution.py
+++ b/solution.py
@@ -257,6 +257,9 @@
         _, buf, _, new, line = pairs[c]
         for i in range(parts):
             copy_in(c, i).wait()
+        if c == 1:
+            for i in range(parts):
+                copy_out(0, i).start()
 
         def prefix(i, carry):
             line[pl.ds(pl.multiple_of(i * page, page), page), :] = buf[table[req0, i]]
@@ -283,8 +286,9 @@
             return carry
 
         lax.fori_loop(0, n_dec, decode, 0, unroll=4)
-        for i in range(parts):
-            copy_out(c, i).start()
+        if c == 1:
+            for i in range(parts):
+                copy_out(1, i).start()
 
     def some_pages(buf, req, t):
         return jnp.concatenate([buf[table[req, t * some + j]] for j in range(some)], axis=0)
@@ -324,7 +328,6 @@
              lambda t: tile_mix(vc, score_buf, top, weight, acc, t, tile, scale))
         close_mix(weight, acc, early.at[e])
 
-    block_scores(ahead[0])
     arrive(1)
 
     def mix(g, carry):
@@ -342,6 +345,7 @@
     lax.fori_loop(0, n_dec // both, mix, 0)
     for n in range(n_q):
         out[:, n * head:(n + 1) * head] = of[n].astype(jnp.bfloat16)
+    block_scores(ahead[0])
     block_mix(ahead[0], 0)
     block_scores(ahead[1])
     block_mix(ahead[1], 1)
@@ -380,8 +384,8 @@
     )(table, reqs, pos, q, kn, vn, kp, vp)
 
 
-def attend_kernel(tp, parts, scale, tile, pre_len, q, dec, early, w_o_any, x_any, g, keys, vals, mid_out, hid_out,
-                  w_o, x, in_sem, score, top, weight, acc, o,
+def attend_kernel(tp, parts, scale, tile, pre_len, q_any, dec, early, w_o_any, x_any, g, keys_any, vals_any, mid_out, hid_out,
+                  w_o, x, q, keys, vals, in_sem, score, top, weight, acc, o,
                   psend, precv, ssend, rrecv, ps_sem, pr_sem, ss_sem, rr_sem):
     chips = tp // 2
     chip, core, peer, chip_at = ring_places(tp)
@@ -392,7 +396,8 @@
     span = keys.shape[0]
     pre_tiles, all_tiles = pre_len // tile, span // tile
     n_dec = dec.shape[0]
-    loads = [pltpu.make_async_copy(w_o_any, w_o, in_sem.at[0]), pltpu.make_async_copy(x_any, x, in_sem.at[1])]
+    loads = [pltpu.make_async_copy(a, b, in_sem.at[i]) for i, (a, b) in enumerate(
+        ((w_o_any, w_o), (q_any, q), (keys_any, keys), (vals_any, vals), (x_any, x)))]
     for load in loads:
         load.start()
     greet(peer, nxt, prv)
@@ -505,13 +510,14 @@
 
         @pl.when(s == 0)
         def _():
+            for load in loads[1:]:
+                load.wait()
             top[0] = jnp.full(top.shape[1:], -jnp.inf, jnp.float32)
             loop(0, tiles(theirs(1)), lambda t: scores(theirs(1), 0, t, True))
 
         return carry
 
-    for load in loads:
-        load.wait()
+    loads[0].wait()
     lax.fori_loop(0, chips, step, 0)
 
     total = score.at[1, 0]
@@ -549,10 +555,10 @@
     return pl.pallas_call(
         functools.partial(attend_kernel, tp, parts, head ** -0.5 * LOG2E, tile, pre_len),
         out_shape=[out, out],
-        in_specs=[VMEM] * 3 + [ANY] * 2 + [VMEM] * 3,
+        in_specs=[ANY, VMEM, VMEM, ANY, ANY, VMEM, ANY, ANY],
         out_specs=[VMEM] * 2,
         scratch_shapes=[
-            pltpu.VMEM(w_o.shape, bf), pltpu.VMEM((rows, d), bf), dma((2,)),
+            pltpu.VMEM(w_o.shape, bf), pltpu.VMEM((rows, d), bf), pltpu.VMEM(q.shape, bf), pltpu.VMEM((span, head), bf), pltpu.VMEM((span, head), bf), dma((5,)),
             pltpu.VMEM((2, n_q, rows, span), f32), pltpu.VMEM((2, n_q, rows, head), f32),
             pltpu.VMEM((n_q, rows, head), f32), pltpu.VMEM((n_q, rows, head), f32),
             pltpu.VMEM((rows, n_q * head), bf),

time: 292 us -> 290 us (level)
  no operation moved by 1% of the time
where the time goes in v4:
time: 290 us
  Pallas kernels  285 us (98%)
  local copies, waits for them, and re-layouts  4.09 us (1%)
    pallas_call x1, Pallas kernels, mlp(): pl.pallas_call(functools.partial(mlp_kernel, tp, parts), out_shape=jax.Sh...  112 us
    pallas_call x1, Pallas kernels, attend_project(): pl.pallas_call(functools.partial(attend_kernel, tp, parts, head ** (-0.5)...  65.1 us
    pallas_call x1, Pallas kernels, front(): pl.pallas_call(functools.partial(front_kernel, tp, start, n_dec), out_sha...  64.3 us
    pallas_call x1, Pallas kernels, cache_and_decode(): pl.pallas_call(functools.partial(cache_kernel, tp, tile, parts, head ** (...  43.7 us

profile of v4, /device:TPU:112, one launch (start us, length us, event | category | flops | bytes accessed | tf_op | source)
XLA Modules:
  0.0 289.9 jit_solution(5124573733185816648)
XLA Ops:
  0.6 0.7 stack.9
  1.3 0.7 stack.10
  2.0 0.6 maximum_convert_fusion.g
  2.7 64.3 %front.1 = (bf16[3,8,264,128]{3,2,1,0:T(8,128)(2,1)}, bf16[8,264,128]{2,1,0:T(8,128)(2,1)}, bf16[8,264,128]{2,1,0:T(8,128)(2,1)}) custom-call(s32[2112]{0:T(1024)} %pos.3, bf16[264,3072]{1,0:T(8,128)(2,1)} %x_any.1, f32[2,3072]{1,0:T(2,128)} %maximum_convert_fusion.g, f32[1,128]{1,0:T(1,128)} %constant.2.clone.freq, bf16[3072,384]{1,0:T(8,128)(2,1)} %w_q.1, ...), custom_call_target="tpu_custom_call" | custom-call | flops 60000002048 | bytes 10000000 | tf_op jit(solution)/shard_map/front/pallas_call | solution.py:151
  66.9 43.7 %cache_and_decode.1 = (bf16[64,384]{1,0:T(8,128)(2,1)}, bf16[4352,16,128]{2,1,0:T(8,128)(2,1)}, bf16[4352,16,128]{2,1,0:T(8,128)(2,1)}, bf16[4096,128]{1,0:T(8,1...) custom-call(s32[65,256]{1,0:T(8,128)} %table.1, s32[2112]{0:T(1024)} %reqs.1, s32[2112]{0:T(1024)} %pos.3, ...), custom_call_target="tpu_custom_call" | custom-call | flops 40000000000 | bytes 100000000 | tf_op jit(solution)/shard_map/cache_and_decode/pallas_call | solution.py:368
  110.6 65.1 %attend_project.1 = (bf16[264,3072]{1,0:T(8,128)(2,1)}, bf16[264,3072]{1,0:T(8,128)(2,1)}) custom-call(bf16[3,8,264,128]{3,2,1,0:T(8,128)(2,1)} %get-tuple-element.14.q.q_any, bf16[64,384]{1,0:T(8,128)(2,1)} %get-tuple-element.17.dec, bf16[2,264,384]{2,1,0:T(8,128)(2,1)} %get-tuple-element.18.early, bf16[384,3072]{1,0:T(8,128)(2,1)} %w_o_any.1, ...), custom_call_target="tpu_custom_call" | custom-call | flops 60000002048 | bytes 10000000 | tf_op jit(solution)/shard_map/attend_project/pallas_call | solution.py:555
  175.7 111.5 %mlp.1 = bf16[264,3072]{1,0:T(8,128)(2,1)} custom-call(bf16[264,3072]{1,0:T(8,128)(2,1)} %get-tuple-element.21.hid, bf16[264,3072]{1,0:T(8,128)(2,1)} %get-tuple-element.22.mid, bf16[3072,1024]{1,0:T(8,128)(2,1)} %w_gate.1, bf16[3072,1024]{1,0:T(8,128)(2,1)} %w_up.1, bf16[1024,3072]{1,0:T(8,128)(2,1)} %w_down.1), custom_call_target="tpu_custom_call" | custom-call | flops 99999997952 | bytes 20000000 | tf_op jit(solution)/shard_map/mlp/pallas_call | solution.py:708
  287.2 2.7 copy.22

commit v5 on v4

--- a/solution.py
+++ b/solution.py
@@ -226,7 +226,7 @@
 
 
 def cache_kernel(tp, tile, parts, scale, pre_pages, dec_pages, table, reqs, pos, q, kn, vn, kp, vp, out, ko, vo, kc, vc, early,
-                 kbuf, vbuf, prob, total, qf, of, score_buf, top, weight, acc, in_sem, out_sem):
+                 kbuf, vbuf, prob, total, qf, of, score_buf, top, weight, acc, in_sem, out_sem, pre_sem):
     n_q, n_dec, head = qf.shape
     rows = q.shape[2]
     chip, core, peer, chip_at = ring_places(tp)
@@ -247,30 +247,31 @@
         at = pl.ds(i * step, step)
         return pltpu.make_async_copy(pairs[c][1].at[at], pairs[c][2].at[at], out_sem.at[c, i])
 
+    pre_len = pre_pages * page
+    span = kc.shape[0]
+    for c, (src, _, _, new, line) in enumerate(pairs):
+
+        def fetch(i, carry, c=c, src=src, line=line):
+            rows = pl.ds(pl.multiple_of(i * page, page), page)
+            pltpu.make_async_copy(src.at[table[reqs[0], i]], line.at[rows, :], pre_sem.at[c]).start()
+            return carry
+
+        lax.fori_loop(0, pre_pages, fetch, 0, unroll=8)
     for c in range(2):
         for i in range(parts):
             copy_in(c, i).start()
+    for c, (_, _, _, new, line) in enumerate(pairs):
+        line[pl.ds(pre_len, chunk_len), :] = new[pl.ds(0, chunk_len), :]
     qf[...] = q[:, tp - 1, pl.ds(rows - n_dec, n_dec), :].astype(jnp.float32)
     req0 = reqs[0]
 
     def arrive(c):
-        _, buf, _, new, line = pairs[c]
+        _, buf, _, new, _ = pairs[c]
         for i in range(parts):
             copy_in(c, i).wait()
-        if c == 1:
-            for i in range(parts):
-                copy_out(0, i).start()
-
-        def prefix(i, carry):
-            line[pl.ds(pl.multiple_of(i * page, page), page), :] = buf[table[req0, i]]
-            return carry
-
-        lax.fori_loop(0, pre_pages, prefix, 0, unroll=8)
 
         def chunk(i, carry):
-            rows = new[pl.ds(pl.multiple_of(i * page, page), page), :]
-            buf[table[req0, pre_pages + i]] = rows
-            line[pl.ds(pl.multiple_of((pre_pages + i) * page, page), page), :] = rows
+            buf[table[req0, pre_pages + i]] = new[pl.ds(pl.multiple_of(i * page, page), page), :]
             return carry
 
         lax.fori_loop(0, chunk_pages, chunk, 0, unroll=8)
@@ -286,9 +287,8 @@
             return carry
 
         lax.fori_loop(0, n_dec, decode, 0, unroll=4)
-        if c == 1:
-            for i in range(parts):
-                copy_out(1, i).start()
+        for i in range(parts):
+            copy_out(c, i).start()
 
     def some_pages(buf, req, t):
         return jnp.concatenate([buf[table[req, t * some + j]] for j in range(some)], axis=0)
@@ -297,7 +297,25 @@
     blank = jnp.zeros((8 - n_q, head), jnp.float32)
     both = 8
 
+    def block_scores(block):
+        top[...] = jnp.full(top.shape, -jnp.inf, jnp.float32)
+        loop(0, tile_count(block, rows, pre_len, span, tile),
+             lambda t: tile_scores(q, kc, score_buf, top, block, t, tile, pre_len, True))
+
+    def block_mix(block, e):
+        open_mix(top, weight, acc)
+        loop(0, tile_count(block, rows, pre_len, span, tile),
+             lambda t: tile_mix(vc, score_buf, top, weight, acc, t, tile, scale))
+        close_mix(weight, acc, early.at[e])
+
+    for c, line in enumerate((kc, vc)):
+        whole = line.at[pl.ds(0, pre_len), :]
+        pltpu.make_async_copy(whole, whole, pre_sem.at[c]).wait()
+    for e in range(2):
+        block_scores(ahead[e])
+        block_mix(ahead[e], e)
     arrive(0)
+    arrive(1)
 
     def score(g, carry):
         for r in range(both):
@@ -314,21 +332,6 @@
         return carry
 
     lax.fori_loop(0, n_dec // both, score, 0)
-    pre_len = pre_pages * page
-    span = kc.shape[0]
-
-    def block_scores(block):
-        top[...] = jnp.full(top.shape, -jnp.inf, jnp.float32)
-        loop(0, tile_count(block, rows, pre_len, span, tile),
-             lambda t: tile_scores(q, kc, score_buf, top, block, t, tile, pre_len, True))
-
-    def block_mix(block, e):
-        open_mix(top, weight, acc)
-        loop(0, tile_count(block, rows, pre_len, span, tile),
-             lambda t: tile_mix(vc, score_buf, top, weight, acc, t, tile, scale))
-        close_mix(weight, acc, early.at[e])
-
-    arrive(1)
 
     def mix(g, carry):
         for r in range(both):
@@ -345,10 +348,6 @@
     lax.fori_loop(0, n_dec // both, mix, 0)
     for n in range(n_q):
         out[:, n * head:(n + 1) * head] = of[n].astype(jnp.bfloat16)
-    block_scores(ahead[0])
-    block_mix(ahead[0], 0)
-    block_scores(ahead[1])
-    block_mix(ahead[1], 1)
     for c in range(2):
         for i in range(parts):
             copy_out(c, i).wait()
@@ -376,7 +375,7 @@
             pltpu.VMEM((n_q, n_dec, head), f32), pltpu.VMEM((n_q, n_dec, head), f32),
             pltpu.VMEM((n_q, rows, line.shape[0]), f32), pltpu.VMEM((n_q, rows, head), f32),
             pltpu.VMEM((n_q, rows, head), f32), pltpu.VMEM((n_q, rows, head), f32),
-            dma((2, parts)), dma((2, parts)),
+            dma((2, parts)), dma((2, parts)), dma((2,)),
         ],
         compiler_params=pltpu.CompilerParams(vmem_limit_bytes=67043328),
         cost_estimate=cost(4e10, 1e8),

time: 290 us -> 285 us (0.983)
  Pallas kernels: 285 us -> 279 us
    pallas_call x1, Pallas kernels: 43.7 us -> 38.3 us  [cache_and_decode(): pl.pallas_call(functools.partial(cache_kernel, tp, tile, parts, head ** (...]
where the time goes in v5:
time: 285 us
  Pallas kernels  279 us (98%)
  local copies, waits for them, and re-layouts  4.09 us (1%)
    pallas_call x1, Pallas kernels, mlp(): pl.pallas_call(functools.partial(mlp_kernel, tp, parts), out_shape=jax.Sh...  112 us
    pallas_call x1, Pallas kernels, attend_project(): pl.pallas_call(functools.partial(attend_kernel, tp, parts, head ** (-0.5)...  65.1 us
    pallas_call x1, Pallas kernels, front(): pl.pallas_call(functools.partial(front_kernel, tp, start, n_dec), out_sha...  64.3 us
    pallas_call x1, Pallas kernels, cache_and_decode(): pl.pallas_call(functools.partial(cache_kernel, tp, tile, parts, head ** (...  38.3 us

profile of v5, /device:TPU:112, one launch (start us, length us, event | category | flops | bytes accessed | tf_op | source)
XLA Modules:
  0.0 284.5 jit_solution(3479050302256354275)
XLA Ops:
  0.6 0.7 stack.9
  1.3 0.7 stack.10
  2.0 0.6 maximum_convert_fusion.g
  2.7 64.3 %front.1 = (bf16[3,8,264,128]{3,2,1,0:T(8,128)(2,1)}, bf16[8,264,128]{2,1,0:T(8,128)(2,1)}, bf16[8,264,128]{2,1,0:T(8,128)(2,1)}) custom-call(s32[2112]{0:T(1024)} %pos.3, bf16[264,3072]{1,0:T(8,128)(2,1)} %x_any.1, f32[2,3072]{1,0:T(2,128)} %maximum_convert_fusion.g, f32[1,128]{1,0:T(1,128)} %constant.2.clone.freq, bf16[3072,384]{1,0:T(8,128)(2,1)} %w_q.1, ...), custom_call_target="tpu_custom_call" | custom-call | flops 60000002048 | bytes 10000000 | tf_op jit(solution)/shard_map/front/pallas_call | solution.py:151
  66.9 38.3 %cache_and_decode.1 = (bf16[64,384]{1,0:T(8,128)(2,1)}, bf16[4352,16,128]{2,1,0:T(8,128)(2,1)}, bf16[4352,16,128]{2,1,0:T(8,128)(2,1)}, bf16[4096,128]{1,0:T(8,1...) custom-call(s32[65,256]{1,0:T(8,128)} %table.1, s32[2112]{0:T(1024)} %reqs.1, s32[2112]{0:T(1024)} %pos.3, ...), custom_call_target="tpu_custom_call" | custom-call | flops 40000000000 | bytes 100000000 | tf_op jit(solution)/shard_map/cache_and_decode/pallas_call | solution.py:367
  105.2 65.1 %attend_project.1 = (bf16[264,3072]{1,0:T(8,128)(2,1)}, bf16[264,3072]{1,0:T(8,128)(2,1)}) custom-call(bf16[3,8,264,128]{3,2,1,0:T(8,128)(2,1)} %get-tuple-element.14.q.q_any, bf16[64,384]{1,0:T(8,128)(2,1)} %get-tuple-element.17.dec, bf16[2,264,384]{2,1,0:T(8,128)(2,1)} %get-tuple-element.18.early, bf16[384,3072]{1,0:T(8,128)(2,1)} %w_o_any.1, ...), custom_call_target="tpu_custom_call" | custom-call | flops 60000002048 | bytes 10000000 | tf_op jit(solution)/shard_map/attend_project/pallas_call | solution.py:554
  170.3 111.5 %mlp.1 = bf16[264,3072]{1,0:T(8,128)(2,1)} custom-call(bf16[264,3072]{1,0:T(8,128)(2,1)} %get-tuple-element.21.hid, bf16[264,3072]{1,0:T(8,128)(2,1)} %get-tuple-element.22.mid, bf16[3072,1024]{1,0:T(8,128)(2,1)} %w_gate.1, bf16[3072,1024]{1,0:T(8,128)(2,1)} %w_up.1, bf16[1024,3072]{1,0:T(8,128)(2,1)} %w_down.1), custom_call_target="tpu_custom_call" | custom-call | flops 99999997952 | bytes 20000000 | tf_op jit(solution)/shard_map/mlp/pallas_call | solution.py:707
  281.8 2.7 copy.22

commit v6 on v5

--- a/solution.py
+++ b/solution.py
@@ -226,7 +226,7 @@
 
 
 def cache_kernel(tp, tile, parts, scale, pre_pages, dec_pages, table, reqs, pos, q, kn, vn, kp, vp, out, ko, vo, kc, vc, early,
-                 kbuf, vbuf, prob, total, qf, of, score_buf, top, weight, acc, in_sem, out_sem, pre_sem):
+                 kbuf, vbuf, qf, of, score_buf, top, weight, acc, in_sem, out_sem, pre_sem):
     n_q, n_dec, head = qf.shape
     rows = q.shape[2]
     chip, core, peer, chip_at = ring_places(tp)
@@ -327,25 +327,15 @@
                 for t in range(dec_pages // some)], axis=1)
             s = jnp.where(col <= pos[chunk_len + i], s, -1e30)
             p = jnp.exp2((s - jnp.max(s, axis=-1, keepdims=True)) * scale)
-            total[i] = jnp.broadcast_to(jnp.sum(p, axis=-1, keepdims=True), (8, head))
-            prob[i] = p
-        return carry
-
-    lax.fori_loop(0, n_dec // both, score, 0)
-
-    def mix(g, carry):
-        for r in range(both):
-            i = g * both + r
-            req = reqs[chunk_len + i]
             o = sum(
-                jnp.dot(prob[i, :, t * wide:(t + 1) * wide].astype(jnp.bfloat16), some_pages(vbuf, req, t), preferred_element_type=jnp.float32)
+                jnp.dot(p[:, t * wide:(t + 1) * wide].astype(jnp.bfloat16), some_pages(vbuf, req, t), preferred_element_type=jnp.float32)
                 for t in range(dec_pages // some))
-            o = o / total[i]
+            o = o / jnp.sum(p, axis=-1, keepdims=True)
             for n in range(n_q):
                 of[n, pl.ds(i, 1), :] = o[n:n + 1]
         return carry
 
-    lax.fori_loop(0, n_dec // both, mix, 0)
+    lax.fori_loop(0, n_dec // both, score, 0)
     for n in range(n_q):
         out[:, n * head:(n + 1) * head] = of[n].astype(jnp.bfloat16)
     for c in range(2):
@@ -371,7 +361,6 @@
         out_specs=[VMEM, ANY, ANY, VMEM, VMEM, VMEM],
         scratch_shapes=[
             pltpu.VMEM(kp.shape, bf), pltpu.VMEM(kp.shape, bf),
-            pltpu.VMEM((n_dec, 8, dec_pages * page), f32), pltpu.VMEM((n_dec, 8, head), f32),
             pltpu.VMEM((n_q, n_dec, head), f32), pltpu.VMEM((n_q, n_dec, head), f32),
             pltpu.VMEM((n_q, rows, line.shape[0]), f32), pltpu.VMEM((n_q, rows, head), f32),
             pltpu.VMEM((n_q, rows, head), f32), pltpu.VMEM((n_q, rows, head), f32),

time: 285 us -> 290 us (1.018)
  Pallas kernels: 279 us -> 285 us
    pallas_call x1, Pallas kernels: 38.3 us -> 43.6 us  [cache_and_decode(): pl.pallas_call(functools.partial(cache_kernel, tp, tile, parts, head ** (...]
where the time goes in v6:
time: 290 us
  Pallas kernels  285 us (98%)
  local copies, waits for them, and re-layouts  4.09 us (1%)
    pallas_call x1, Pallas kernels, mlp(): pl.pallas_call(functools.partial(mlp_kernel, tp, parts), out_shape=jax.Sh...  112 us
    pallas_call x1, Pallas kernels, attend_project(): pl.pallas_call(functools.partial(attend_kernel, tp, parts, head ** (-0.5)...  65.1 us
    pallas_call x1, Pallas kernels, front(): pl.pallas_call(functools.partial(front_kernel, tp, start, n_dec), out_sha...  64.3 us
    pallas_call x1, Pallas kernels, cache_and_decode(): pl.pallas_call(functools.partial(cache_kernel, tp, tile, parts, head ** (...  43.6 us

profile of v6, /device:TPU:112, one launch (start us, length us, event | category | flops | bytes accessed | tf_op | source)
XLA Modules:
  0.0 290.1 jit_solution(8041702422772376249)
XLA Ops:
  0.6 0.7 stack.9
  1.3 0.7 stack.10
  2.0 0.6 maximum_convert_fusion.g
  2.7 64.3 %front.1 = (bf16[3,8,264,128]{3,2,1,0:T(8,128)(2,1)}, bf16[8,264,128]{2,1,0:T(8,128)(2,1)}, bf16[8,264,128]{2,1,0:T(8,128)(2,1)}) custom-call(s32[2112]{0:T(1024)} %pos.3, bf16[264,3072]{1,0:T(8,128)(2,1)} %x_any.1, f32[2,3072]{1,0:T(2,128)} %maximum_convert_fusion.g, f32[1,128]{1,0:T(1,128)} %constant.2.clone.freq, bf16[3072,384]{1,0:T(8,128)(2,1)} %w_q.1, ...), custom_call_target="tpu_custom_call" | custom-call | flops 60000002048 | bytes 10000000 | tf_op jit(solution)/shard_map/front/pallas_call | solution.py:151
  66.9 43.6 %cache_and_decode.1 = (bf16[64,384]{1,0:T(8,128)(2,1)}, bf16[4352,16,128]{2,1,0:T(8,128)(2,1)}, bf16[4352,16,128]{2,1,0:T(8,128)(2,1)}, bf16[4096,128]{1,0:T(8,1...) custom-call(s32[65,256]{1,0:T(8,128)} %table.1, s32[2112]{0:T(1024)} %reqs.1, s32[2112]{0:T(1024)} %pos.3, ...), custom_call_target="tpu_custom_call" | custom-call | flops 40000000000 | bytes 100000000 | tf_op jit(solution)/shard_map/cache_and_decode/pallas_call | solution.py:357
  110.6 65.1 %attend_project.1 = (bf16[264,3072]{1,0:T(8,128)(2,1)}, bf16[264,3072]{1,0:T(8,128)(2,1)}) custom-call(bf16[3,8,264,128]{3,2,1,0:T(8,128)(2,1)} %get-tuple-element.14.q.q_any, bf16[64,384]{1,0:T(8,128)(2,1)} %get-tuple-element.17.dec, bf16[2,264,384]{2,1,0:T(8,128)(2,1)} %get-tuple-element.18.early, bf16[384,3072]{1,0:T(8,128)(2,1)} %w_o_any.1, ...), custom_call_target="tpu_custom_call" | custom-call | flops 60000002048 | bytes 10000000 | tf_op jit(solution)/shard_map/attend_project/pallas_call | solution.py:543
  175.6 111.7 %mlp.1 = bf16[264,3072]{1,0:T(8,128)(2,1)} custom-call(bf16[264,3072]{1,0:T(8,128)(2,1)} %get-tuple-element.21.hid, bf16[264,3072]{1,0:T(8,128)(2,1)} %get-tuple-element.22.mid, bf16[3072,1024]{1,0:T(8,128)(2,1)} %w_gate.1, bf16[3072,1024]{1,0:T(8,128)(2,1)} %w_up.1, bf16[1024,3072]{1,0:T(8,128)(2,1)} %w_down.1), custom_call_target="tpu_custom_call" | custom-call | flops 99999997952 | bytes 20000000 | tf_op jit(solution)/shard_map/mlp/pallas_call | solution.py:696
  287.4 2.7 copy.22
